TPU v7x, 32 devices: a whole 2x2x4 slice. The times are simulated.
32 devices in a mesh: groups: 2 (over y), dom: 8 (over z, core), tilt: 2 (over x), rep: 1.
Axes of the slice: x: 2, y: 2, z: 4, core: 2. Of those that a mesh axis runs over, the one named last changes fastest.
Arguments:
- patches: bfloat16 [4, 1024, 128, 128], P(('groups', 'tilt'), 'dom'), parts along dimension 0, may hold values from -6 to 6
- slot_view: int32 [4, 1024, 1], P(('groups', 'tilt'), 'dom'), parts along dimension 0, may hold values from 0 to 31, as said below
- slot_tilt: int32 [4, 1024], P(('groups', 'tilt'), 'dom'), parts along dimension 0, may hold values from 0 to 9
- slot_pos: bfloat16 [2, 4, 1024], P(None, ('groups', 'tilt'), 'dom'), parts along dimension 1, may hold values from 0 to 1
- defocus: bfloat16 [4, 1024], P(('groups', 'tilt'), 'dom'), parts along dimension 0, may hold values from 1 to 3
- projections: bfloat16 [64, 20, 2, 128, 128], P(('groups', 'dom'), 'tilt', None, 'rep'), parts along dimension 0, may hold values from -6 to 6
- warp_grid: float32 [40, 2, 256], P(('groups', 'tilt')), parts along dimension 0, may hold values from -6 to 6
Outputs:
- slot_terms: float32 [3, 4, 1024], P(None, ('groups', 'tilt'), 'dom'), parts along dimension 1
- new_warp: float32 [40, 2, 256], P(('groups', 'tilt')), parts along dimension 0
There are 2 independent parts, one for each index of `groups`. A program takes and returns all parts, laid end to end along the dimension named above; each array names one. Nothing has to cross between parts.
Inputs may be any that keep to these rules, and one draw needn't show every extreme that they name: `slot_view`: view v is owned by dom index v // 4. Among the 128 slots of one device (one tilt index and one dom index) at most 24 name views of any one owner, and in every such block some owner is named exactly 24 times.
All inputs are finite; a program needn't handle non-finite values.
Results may differ from a plain program's by a relative error of at most 0.0018.
Values may be sent and summed in bfloat16 or wider, within the bound.
A program may use at most 64 MiB of HBM per device.

v0:
```python
import functools
import math

import jax
import jax.numpy as jnp
from jax import lax
from jax.experimental import pallas as pl
from jax.experimental.pallas import tpu as pltpu
from jax.sharding import PartitionSpec as P

GRID = 16


AMPLITUDE = 0.07
TRUST_FLOOR = 0.02


def signed_freq(index, pixels):
    return jnp.where(index < pixels // 2, index, index - pixels).astype(jnp.float32)


def dft_tables(freq_rows, pixels):
    columns = jnp.arange(pixels, dtype=jnp.int32)
    table_scale = 1.0 / math.sqrt(pixels)
    turns_rows = (freq_rows[:, None] * columns[None, :] % pixels).astype(jnp.float32) * (
        2.0 * math.pi / pixels
    )
    turns_full = (columns[:, None] * columns[None, :] % pixels).astype(jnp.float32) * (
        2.0 * math.pi / pixels
    )
    row_table = jnp.concatenate([jnp.cos(turns_rows), jnp.sin(turns_rows)], axis=0) * table_scale
    col_table = jnp.concatenate([jnp.cos(turns_full), jnp.sin(turns_full)], axis=1) * table_scale
    return (row_table.astype(jnp.bfloat16), col_table.astype(jnp.bfloat16))


def node_weights(pos_x, pos_y, grid_side):
    knot_pos = jnp.arange(grid_side, dtype=jnp.int32).astype(jnp.float32)
    weight_x = jnp.maximum(0.0, 1.0 - jnp.abs(pos_x[:, None] * (grid_side - 1) - knot_pos[None, :]))
    weight_y = jnp.maximum(0.0, 1.0 - jnp.abs(pos_y[:, None] * (grid_side - 1) - knot_pos[None, :]))
    return (weight_y[:, :, None] * weight_x[:, None, :]).reshape(
        pos_x.shape[0], grid_side * grid_side
    )


def spectral_terms(spectrum, ref_blk, focus_blk, shift_blk, freq_rows, pixels):
    row_total = freq_rows.shape[0]
    v_one_cos = spectrum[:, :row_total, :pixels]
    v_one_sin = spectrum[:, :row_total, pixels:]
    v_two_cos = spectrum[:, row_total:, :pixels]
    v_two_sin = spectrum[:, row_total:, pixels:]
    real_part = v_one_cos - v_two_sin
    imag_part = -(v_one_sin + v_two_cos)
    freq_y = signed_freq(freq_rows, pixels)[None, :, None]
    freq_x = signed_freq(jnp.arange(pixels, dtype=jnp.int32), pixels)[None, None, :]
    nyquist = pixels / 2.0
    radius = (freq_y * freq_y + freq_x * freq_x) / (nyquist * nyquist)
    aberration = math.pi * focus_blk[:, None, None] * radius
    contrast = -(
        math.sqrt(1.0 - AMPLITUDE * AMPLITUDE) * jnp.sin(aberration)
        + AMPLITUDE * jnp.cos(aberration)
    )
    phase_angle = (
        2.0
        * math.pi
        / pixels
        * (freq_x * shift_blk[:, 0, None, None] + freq_y * shift_blk[:, 1, None, None])
    )
    cosine = jnp.cos(phase_angle)
    sine_part = jnp.sin(phase_angle)
    ref_real = ref_blk[:, 0].astype(jnp.float32)
    ref_imag = ref_blk[:, 1].astype(jnp.float32)
    model_real = contrast * (ref_real * cosine + ref_imag * sine_part)
    model_imag = contrast * (ref_imag * cosine - ref_real * sine_part)
    diff_real = real_part - model_real
    diff_imag = imag_part - model_imag
    inverse_area = 1.0 / (pixels * pixels)
    energy = jnp.sum(diff_real * diff_real + diff_imag * diff_imag, axis=(1, 2)) * inverse_area
    cross_term = diff_imag * model_real - diff_real * model_imag
    grad_x = 2.0 * inverse_area * jnp.sum(2.0 * math.pi / pixels * freq_x * cross_term, axis=(1, 2))
    grad_y = 2.0 * inverse_area * jnp.sum(2.0 * math.pi / pixels * freq_y * cross_term, axis=(1, 2))
    return jnp.stack([energy, grad_x, grad_y], axis=1)


def on_device(patches, slot_view, slot_tilt, slot_pos, defocus, projections, warp_grid):
    owners = lax.axis_size("dom")
    slot_count = patches.shape[1]
    pixels = patches.shape[-1]
    view_dev = projections.shape[0]
    tilt_dev = warp_grid.shape[0]
    node_count = warp_grid.shape[2]
    capacity = 3 * slot_count // (2 * owners)
    buffer_len = owners * capacity
    chosen_view = slot_view[0, :, 0]
    owner_of = chosen_view // view_dev
    owner_hits = (owner_of[:, None] == jnp.arange(owners, dtype=jnp.int32)[None, :]).astype(
        jnp.int32
    )
    earlier = jnp.cumsum(owner_hits, axis=0) - owner_hits
    slot_rank = jnp.sum(earlier * owner_hits, axis=1)
    target = owner_of * capacity + slot_rank
    matches = target[None, :] == jnp.arange(buffer_len, dtype=jnp.int32)[:, None]
    source = jnp.sum(
        jnp.where(matches, jnp.arange(slot_count, dtype=jnp.int32)[None, :], 0), axis=1
    )
    filled = jnp.any(matches, axis=1)
    patch_rows = jnp.where(filled[:, None, None], patches[0][source], jnp.zeros((), jnp.bfloat16))
    slot_meta = jnp.stack(
        [
            slot_tilt[0].astype(jnp.float32),
            (chosen_view % view_dev).astype(jnp.float32),
            defocus[0].astype(jnp.float32),
            slot_pos[0, 0].astype(jnp.float32),
            slot_pos[1, 0].astype(jnp.float32),
            jnp.ones((slot_count,), jnp.float32),
        ],
        axis=1,
    )
    meta_rows = jnp.where(filled[:, None], slot_meta[source], 0.0).astype(jnp.bfloat16)
    patch_buffer = patch_rows.reshape(owners, capacity, pixels, pixels)
    meta_buffer = meta_rows.reshape(owners, capacity, 6)
    row_span = projections.shape[3]
    freq_rows = lax.axis_index("rep") * row_span + jnp.arange(row_span, dtype=jnp.int32)
    row_table, col_table = dft_tables(freq_rows, pixels)
    row_total = freq_rows.shape[0]
    projected_flat = projections.reshape(view_dev * tilt_dev, 2, row_total, pixels)
    tilt_iota = jnp.arange(tilt_dev, dtype=jnp.int32)
    view_iota = jnp.arange(view_dev, dtype=jnp.int32)

    def one_block(inputs):
        patch_blk, index_blk, focus_blk, shift_blk = inputs
        ref_blk = projected_flat[index_blk]
        first_pass = jnp.einsum(
            "fy,byx->bfx", row_table, patch_blk, preferred_element_type=jnp.float32
        ).astype(jnp.bfloat16)
        spectrum = jnp.einsum(
            "bfx,xk->bfk", first_pass, col_table, preferred_element_type=jnp.float32
        )
        return spectral_terms(spectrum, ref_blk, focus_blk, shift_blk, freq_rows, pixels)

    patch_in = lax.all_to_all(patch_buffer, "dom", split_axis=0, concat_axis=0, tiled=True)
    meta_in = lax.all_to_all(meta_buffer, "dom", split_axis=0, concat_axis=0, tiled=True)
    senders = patch_in.shape[0]
    per_sender = patch_in.shape[1]
    slot_total = senders * per_sender
    meta_flat = meta_in.reshape(slot_total, 6).astype(jnp.float32)
    tilt_match = meta_flat[:, 0:1] == tilt_iota.astype(jnp.float32)[None, :]
    view_match = meta_flat[:, 1:2] == view_iota.astype(jnp.float32)[None, :]
    tilt_local = jnp.sum(jnp.where(tilt_match, tilt_iota[None, :], 0), axis=1)
    view_local = jnp.sum(jnp.where(view_match, view_iota[None, :], 0), axis=1)
    weights = node_weights(meta_flat[:, 3], meta_flat[:, 4], GRID)
    shifts = jnp.sum(warp_grid[tilt_local] * weights[:, None, :], axis=2)
    block_len = math.gcd(slot_total, 16)
    block_count = slot_total // block_len
    per_slot = lax.map(
        one_block,
        (
            patch_in.reshape(block_count, block_len, pixels, pixels),
            (view_local * tilt_dev + tilt_local).reshape(block_count, block_len),
            meta_flat[:, 2].reshape(block_count, block_len),
            shifts.reshape(block_count, block_len, 2),
        ),
    ).reshape(slot_total, 3)
    node_coef = (
        tilt_match.astype(jnp.float32)[:, :, None]
        * per_slot[:, None, 1:3]
        * meta_flat[:, 5, None, None]
    ).reshape(senders, per_sender, 2 * tilt_dev)
    returned = lax.all_to_all(
        per_slot.reshape(senders, per_sender, 3), "dom", split_axis=0, concat_axis=0, tiled=True
    )
    weight_all = weights.reshape(senders, per_sender, node_count)
    own_terms = returned.reshape(buffer_len, 3)[target]
    summed = lax.psum(own_terms, "rep")
    slot_terms = summed.T[:, None, :]
    gradient = jnp.dot(
        node_coef.reshape(-1, 2 * tilt_dev).T,
        weight_all.reshape(-1, node_count),
        precision=lax.Precision.HIGHEST,
        preferred_element_type=jnp.float32,
    ).reshape(tilt_dev, 2, node_count)
    whole_grad = lax.psum(gradient, ("dom", "rep"))
    new_warp = warp_grid - whole_grad / jnp.sqrt(
        whole_grad * whole_grad + TRUST_FLOOR * TRUST_FLOOR
    )
    return (slot_terms, new_warp)


CORES = 2
EXTRA_ROWS = 8
DELTA = math.asin(AMPLITUDE)
F32 = jnp.float32
BF16 = jnp.bfloat16


def fold_kernel(refs_ref, pick_ref, turn_ref, unit_ref, waves_ref, weights_ref, out_ref):
    pixels = turn_ref.shape[0]
    half = pixels // 2
    lane = lax.broadcasted_iota(jnp.int32, (1, pixels), 1)
    sign = jnp.where(lane < half, 1.0, -1.0)

    def one(n, carry):
        real, imag = refs_ref[n, 0], refs_ref[n, 1]
        wide = jnp.concatenate([real, imag], axis=1)
        picked = jnp.dot(wide, pick_ref[...], preferred_element_type=F32)
        mirrored = picked[:, pixels:]
        turned = jnp.dot(turn_ref[...], mirrored.astype(BF16), preferred_element_type=F32)
        out_ref[n, :pixels] = (picked[:, :pixels] + sign * turned).astype(BF16)
        tall = jnp.concatenate([real, imag], axis=0)
        column = lax.dot_general(
            unit_ref[...], tall, (((1,), (1,)), ((), ())), preferred_element_type=F32
        )
        r, i = real.astype(F32), imag.astype(F32)
        power = r * r + i * i
        mixed = jnp.dot(power.astype(BF16), waves_ref[...], preferred_element_type=F32)
        swing = jnp.sum(mixed * weights_ref[...], axis=0, keepdims=True)
        swing = swing[:, : 2 * pixels] + swing[:, 2 * pixels :]
        total = 0.5 * jnp.sum(power) - 0.5 * swing
        high = total.astype(BF16).astype(F32)
        low = total - high
        extra = jnp.concatenate(
            [
                column[0:1, :pixels],
                column[0:1, pixels:],
                mirrored[half : half + 1],
                high[:, :pixels],
                high[:, pixels:],
                low[:, :pixels],
                low[:, pixels:],
                jnp.zeros((EXTRA_ROWS - 7, pixels), F32),
            ],
            axis=0,
        )
        out_ref[n, pixels:] = extra.astype(BF16)
        return carry

    lax.fori_loop(0, refs_ref.shape[0], one, 0, unroll=True)


def fold_references(projections, pixels):
    half = pixels // 2
    refs = projections.reshape(-1, 2, pixels, pixels)
    count = refs.shape[0]
    k = jnp.arange(pixels, dtype=jnp.int32)
    lane_freq = k % half
    lane_part = k // half
    chan = jnp.arange(2, dtype=jnp.int32)
    same_part = chan[:, None, None] == lane_part[None, None, :]
    pick = same_part & (k[None, :, None] == lane_freq[None, None, :])
    flip = (
        same_part
        & (k[None, :, None] == pixels - lane_freq[None, None, :])
        & (lane_freq > 0)[None, None, :]
    )
    picks = jnp.concatenate([pick, flip], axis=2).reshape(2 * pixels, 2 * pixels).astype(BF16)
    turn = (((k[:, None] + k[None, :]) % pixels == 0) & (k != half)[:, None]).astype(BF16)
    unit = jnp.broadcast_to((k == half).astype(BF16)[None, :], (16, pixels))
    table = jnp.arange(2 * pixels, dtype=jnp.int32)
    focus = jnp.where(
        table < pixels, 1.0 + table / pixels, 2.0 + (table - pixels) / (pixels // 2)
    ).astype(F32)
    freq = signed_freq(k, pixels)
    chi = math.pi * focus[None, :] * (freq * freq / (half * half))[:, None]
    chi = jnp.concatenate([chi, chi + 0.25 * math.pi], axis=1) * 2.0
    waves = jnp.cos(jnp.concatenate([chi[:, : 2 * pixels], chi[:, 2 * pixels :] - math.pi], axis=1))
    weights = jnp.cos(chi + 2.0 * DELTA)
    rows = pixels + EXTRA_ROWS
    group = math.gcd(count, 5)
    full = lambda x: pl.BlockSpec(x.shape, lambda i: (0, 0))
    tables = (picks, turn, unit, waves.astype(BF16), weights)
    return pl.pallas_call(
        fold_kernel,
        grid=(count // group,),
        out_shape=jax.ShapeDtypeStruct((count, rows, pixels), BF16),
        in_specs=[pl.BlockSpec((group, 2, pixels, pixels), lambda i: (i, 0, 0, 0))]
        + [full(x) for x in tables],
        out_specs=pl.BlockSpec((group, rows, pixels), lambda i: (i, 0, 0)),
        name="fold_references",
    )(refs, *tables)


def gather_kernel(chips, cap, src_ref, which_ref, own_ref, patch_ref, meta_ref, first_ref,
                  second_ref, nyq_ref, sums_ref, extra_ref, factor_ref, *rest):
    lefts, rights = rest[: chips - 1], rest[chips - 1 : 2 * chips - 2]
    left_pairs, right_pairs = rest[2 * chips - 2 : 3 * chips - 3], rest[3 * chips - 3 : 4 * chips - 4]
    (pair_ref, rs, rr, ls, lr, lps, lpr, rps, rpr, ps, pr) = rest[4 * chips - 4 :]
    pixels = patch_ref.shape[1]
    half = pixels // 2
    me = lax.axis_index("dom")
    chip = me // CORES
    core = me % CORES
    partner = chip * CORES + (1 - core)
    right = me + CORES
    left = me - CORES
    last = chips - 1
    barrier = pltpu.get_barrier_semaphore()

    def greet(device):
        pl.semaphore_signal(
            barrier, inc=1, device_id={"dom": device}, device_id_type=pl.DeviceIdType.MESH
        )

    greet(partner)

    @pl.when(chip < last)
    def _():
        greet(right)

    @pl.when(chip > 0)
    def _():
        greet(left)

    inner = (chip > 0) & (chip < last)

    @pl.when(inner)
    def _():
        pl.semaphore_wait(barrier, 3)

    @pl.when(jnp.logical_not(inner))
    def _():
        pl.semaphore_wait(barrier, 2)

    def copy(src, dst, send, recv, target):
        return pltpu.make_async_remote_copy(
            src_ref=src, dst_ref=dst, send_sem=send, recv_sem=recv,
            device_id={"dom": target}, device_id_type=pl.DeviceIdType.MESH,
        )

    def to_right(hop):
        src = own_ref if hop == 0 else lefts[hop - 1]
        return copy(src, lefts[hop], rs.at[hop], rr.at[hop], right)

    def to_left(hop):
        src = own_ref if hop == 0 else rights[hop - 1]
        return copy(src, rights[hop], ls.at[hop], lr.at[hop], left)

    def pair_left(hop):
        return copy(lefts[hop], left_pairs[hop], lps.at[hop], lpr.at[hop], partner)

    def pair_right(hop):
        return copy(rights[hop], right_pairs[hop], rps.at[hop], rpr.at[hop], partner)

    pair_own = copy(own_ref, pair_ref, ps, pr, partner)

    @pl.when(chip < last)
    def _():
        to_right(0).start()

    @pl.when(chip > 0)
    def _():
        to_left(0).start()

    pair_own.start()

    row_index = lax.broadcasted_iota(jnp.int32, (pixels, pixels), 0)
    freq_y = jnp.where(row_index < half, row_index, row_index - pixels).astype(F32)
    lane = lax.broadcasted_iota(jnp.int32, (cap, pixels), 1)
    line_y = jnp.where(lane < half, lane, lane - pixels).astype(F32)
    line_x = jnp.where(lane < half, lane, lane - half).astype(F32)
    norm = 1.0 / (half * half)
    step_angle = 2.0 * math.pi / pixels

    def factors(block, carry):
        rows = pl.ds(pl.multiple_of(block * cap, 8), cap)
        focus, shift_x, shift_y = meta_ref[0, rows], meta_ref[1, rows], meta_ref[2, rows]
        chi_y = math.pi * focus * (line_y * line_y * norm) + DELTA
        chi_x = math.pi * focus * (line_x * line_x * norm)
        phi_y = step_angle * shift_y * line_y
        phi_x = step_angle * shift_x * line_x
        s_y, c_y, p_y, q_y = jnp.sin(chi_y), jnp.cos(chi_y), jnp.cos(phi_y), jnp.sin(phi_y)
        c_x, s_x, p_x, q_x = jnp.cos(chi_x), jnp.sin(chi_x), jnp.cos(phi_x), jnp.sin(phi_x)
        values = (s_y * p_y, s_y * q_y, c_y * p_y, c_y * q_y,
                  c_x * p_x, c_x * q_x, s_x * p_x, s_x * q_x)
        for place, value in enumerate(values):
            factor_ref[rows, place] = value
        return carry

    lax.fori_loop(0, meta_ref.shape[1] // cap, factors, 0)

    def process(refs_ref, owner):
        def pair(step, carry):
            base = owner * cap + step * 2
            both = jnp.concatenate(
                [patch_ref[src_ref[base]], patch_ref[src_ref[base + 1]]], axis=1
            )
            first = jnp.dot(first_ref[...], both, preferred_element_type=F32).astype(BF16)
            for part in range(2):
                slot = base + part
                which = which_ref[slot]
                mine = first[:, part * pixels : (part + 1) * pixels]
                wide = jnp.concatenate([mine[:pixels], mine[pixels:]], axis=1)
                spectrum = jnp.dot(wide, second_ref[...], preferred_element_type=F32)
                line = lax.dot_general(
                    nyq_ref[...], mine, (((1,), (1,)), ((), ())), preferred_element_type=F32
                )
                factor = factor_ref[slot]
                a, b, c, d = factor[4:5], factor[5:6], factor[6:7], factor[7:8]
                cols = factor[0:4]
                rows = jnp.concatenate(
                    [
                        jnp.concatenate([-a, b, -c, d], axis=0),
                        jnp.concatenate([-b, -a, -d, -c], axis=0),
                    ],
                    axis=1,
                )
                col_high = cols.astype(BF16).astype(F32)
                row_high = rows.astype(BF16).astype(F32)
                col_low, row_low = cols - col_high, rows - row_high
                col_all = jnp.concatenate(
                    [col_high, col_high, col_low, jnp.zeros_like(col_low)], axis=0
                ).astype(BF16)
                row_all = jnp.concatenate(
                    [row_high, row_low, row_high, jnp.zeros_like(row_low)], axis=0
                ).astype(BF16)
                turn = lax.dot_general(
                    col_all, row_all, (((0,), (0,)), ((), ())), preferred_element_type=F32
                )
                ref = refs_ref[which, :pixels].astype(F32)
                plain = spectrum[:, :pixels]
                along = plain * ref
                across = spectrum[:, pixels:] * ref
                cosine = turn[:, :pixels]
                sine = turn[:, pixels:]
                real = cosine * along - sine * across
                imag = sine * along + cosine * across
                sums_ref[slot] = jnp.concatenate(
                    [
                        jnp.sum(real, axis=0, keepdims=True),
                        jnp.sum(imag, axis=0, keepdims=True),
                        jnp.sum(imag * freq_y, axis=0, keepdims=True),
                        jnp.sum(plain * plain, axis=0, keepdims=True),
                        plain[half : half + 1],
                        line[0:1, :pixels],
                        line[0:1, pixels:],
                        jnp.zeros((1, pixels), F32),
                    ],
                    axis=0,
                )
                extra_ref[slot] = refs_ref[which, pixels:].astype(F32)
            return carry

        lax.fori_loop(0, cap // 2, pair, 0)

    process(own_ref, me)
    pair_own.wait_recv()
    process(pair_ref, partner)
    for hop in range(1, chips):
        @pl.when(chip >= hop)
        def _():
            to_right(hop - 1).wait_recv()
            if hop < last:
                @pl.when(chip < last)
                def _():
                    to_right(hop).start()
            pair_left(hop - 1).start()

        @pl.when(chip + hop <= last)
        def _():
            to_left(hop - 1).wait_recv()
            if hop < last:
                @pl.when(chip > 0)
                def _():
                    to_left(hop).start()
            pair_right(hop - 1).start()

        @pl.when(chip >= hop)
        def _():
            process(lefts[hop - 1], me - CORES * hop)
            pair_left(hop - 1).wait_recv()
            process(left_pairs[hop - 1], partner - CORES * hop)

        @pl.when(chip + hop <= last)
        def _():
            process(rights[hop - 1], me + CORES * hop)
            pair_right(hop - 1).wait_recv()
            process(right_pairs[hop - 1], partner + CORES * hop)

    pair_own.wait_send()
    for hop in range(last):
        @pl.when((chip >= hop) & (chip < last))
        def _():
            to_right(hop).wait_send()

        @pl.when((chip + hop <= last) & (chip > 0))
        def _():
            to_left(hop).wait_send()

        @pl.when(chip >= hop + 1)
        def _():
            pair_left(hop).wait_send()

        @pl.when(chip + hop + 1 <= last)
        def _():
            pair_right(hop).wait_send()


def gather_sums(cap, src, which, own, patches, meta, first, second, nyquist):
    chips = lax.axis_size("dom") // CORES
    pixels = patches.shape[1]
    padded = src.shape[0]
    vmem = pl.BlockSpec(memory_space=pltpu.VMEM)
    smem = pl.BlockSpec(memory_space=pltpu.SMEM)
    dma = pltpu.SemaphoreType.DMA((chips,))
    return pl.pallas_call(
        functools.partial(gather_kernel, chips, cap),
        out_shape=(
            jax.ShapeDtypeStruct((padded, 8, pixels), F32),
            jax.ShapeDtypeStruct((padded, EXTRA_ROWS, pixels), F32),
        ),
        in_specs=[smem, smem] + [vmem] * 6,
        out_specs=(vmem, vmem),
        scratch_shapes=[pltpu.VMEM((padded, 8, pixels), F32)]
        + [pltpu.VMEM(own.shape, own.dtype)] * (4 * (chips - 1) + 1)
        + [dma] * 8
        + [pltpu.SemaphoreType.DMA] * 2,
        compiler_params=pltpu.CompilerParams(
            collective_id=0, has_side_effects=True, vmem_limit_bytes=56 * 1024 * 1024
        ),
        name="gather_sums",
    )(src, which, own, patches, meta, first, second, nyquist)


def step_kernel(owners, grad_ref, warp_ref, out_ref, held_ref, send_sem, recv_sem):
    me = lax.axis_index("dom")
    barrier = pltpu.get_barrier_semaphore()
    for hop in range(1, owners):
        pl.semaphore_signal(
            barrier, inc=1, device_id={"dom": lax.rem(me + hop, owners)},
            device_id_type=pl.DeviceIdType.MESH,
        )
    pl.semaphore_wait(barrier, owners - 1)

    def copy(hop):
        return pltpu.make_async_remote_copy(
            src_ref=grad_ref, dst_ref=held_ref.at[hop - 1], send_sem=send_sem.at[hop - 1],
            recv_sem=recv_sem.at[hop - 1], device_id={"dom": lax.rem(me + hop, owners)},
            device_id_type=pl.DeviceIdType.MESH,
        )

    for hop in range(1, owners):
        copy(hop).start()
    for hop in range(1, owners):
        copy(hop).wait()
    total = grad_ref[...]
    for hop in range(1, owners):
        total = total + held_ref[hop - 1]
    out_ref[...] = warp_ref[...] - total / jnp.sqrt(total * total + TRUST_FLOOR * TRUST_FLOOR)


def warp_step(gradient, warp):
    owners = lax.axis_size("dom")
    vmem = pl.BlockSpec(memory_space=pltpu.VMEM)
    dma = pltpu.SemaphoreType.DMA((owners - 1,))
    return pl.pallas_call(
        functools.partial(step_kernel, owners),
        out_shape=jax.ShapeDtypeStruct(warp.shape, F32),
        in_specs=[vmem, vmem],
        out_specs=vmem,
        scratch_shapes=[pltpu.VMEM((owners - 1,) + warp.shape, F32), dma, dma],
        compiler_params=pltpu.CompilerParams(collective_id=1, has_side_effects=True),
        name="warp_step",
    )(gradient, warp)


def pass_tables(pixels):
    half = pixels // 2
    row_table, col_table = dft_tables(jnp.arange(pixels, dtype=jnp.int32), pixels)
    cosine = col_table[:, :half]
    sine = col_table[:, pixels : pixels + half]
    real = jnp.concatenate([cosine, -sine], axis=0)
    imag = jnp.concatenate([-sine, -cosine], axis=0)
    second = jnp.concatenate([real, imag, imag, -real], axis=1)
    nyquist = jnp.broadcast_to(col_table[:, half][None, :], (16, pixels))
    return row_table, second, nyquist


def line_terms(spec_re, spec_im, ref_re, ref_im, chi, phi):
    contrast = -jnp.sin(chi + DELTA)
    cosine = jnp.cos(phi)
    sine = jnp.sin(phi)
    model_re = contrast * (ref_re * cosine + ref_im * sine)
    model_im = contrast * (ref_im * cosine - ref_re * sine)
    return spec_re * model_re + spec_im * model_im, spec_im * model_re - spec_re * model_im


def finish_terms(sums, extra, focus, shifts, pixels):
    half = pixels // 2
    k = jnp.arange(pixels, dtype=jnp.int32)
    freq = signed_freq(k, pixels)
    lane_freq = (k % half).astype(F32)
    step = 2.0 * math.pi / pixels
    norm = 1.0 / (half * half)
    match = jnp.sum(sums[:, 0], axis=1)
    grad_x = jnp.sum(sums[:, 1] * lane_freq, axis=1)
    grad_y = jnp.sum(sums[:, 2], axis=1)
    power = jnp.sum(sums[:, 3] * jnp.where(lane_freq > 0, 2.0, 1.0), axis=1)
    d = focus[:, None]
    s_x, s_y = shifts[:, 0:1], shifts[:, 1:2]
    col_re, col_im = sums[:, 5], -sums[:, 6]
    power = power + jnp.sum(col_re * col_re + col_im * col_im, axis=1)
    along, across = line_terms(
        col_re, col_im, extra[:, 0], extra[:, 1],
        math.pi * d * (freq * freq * norm + 1.0), step * (freq * s_y - half * s_x),
    )
    match = match + jnp.sum(along, axis=1)
    grad_x = grad_x - half * jnp.sum(across, axis=1)
    grad_y = grad_y + jnp.sum(across * freq, axis=1)
    f = lane_freq[:half]
    along, across = line_terms(
        sums[:, 4, :half], -sums[:, 4, half:], extra[:, 2, :half], extra[:, 2, half:],
        math.pi * d * (f * f * norm + 1.0), step * (-f * s_x - half * s_y),
    )
    match = match + jnp.sum(along, axis=1)
    grad_x = grad_x - jnp.sum(across * f, axis=1)
    grad_y = grad_y - half * jnp.sum(across, axis=1)
    place = jnp.where(
        focus < 2.0, (focus - 1.0) * pixels, pixels + (focus - 2.0) * half
    )
    table_high = extra[:, 3:5].reshape(-1, 2 * pixels)
    table_low = extra[:, 5:7].reshape(-1, 2 * pixels)
    hit = place[:, None] == jnp.arange(2 * pixels, dtype=jnp.int32).astype(F32)[None, :]
    model_power = jnp.sum(jnp.where(hit, table_high + table_low, 0.0), axis=1)
    area = 1.0 / (pixels * pixels)
    energy = (power + model_power - 2.0 * match) * area
    return jnp.stack([energy, 2.0 * area * step * grad_x, 2.0 * area * step * grad_y], axis=0)


def on_device_gathered(
    patches, slot_view, slot_tilt, slot_pos, defocus, projections, warp_grid
):
    owners = lax.axis_size("dom")
    pixels = patches.shape[-1]
    slots = patches.shape[1]
    view_dev = projections.shape[0]
    tilt_dev = warp_grid.shape[0]
    node_count = warp_grid.shape[2]
    cap = 3 * slots // (2 * owners)
    padded = owners * cap
    exact = functools.partial(
        jnp.dot, precision=lax.Precision.HIGHEST, preferred_element_type=F32
    )
    own = fold_references(projections, pixels)
    tilt = slot_tilt[0]
    view = slot_view[0, :, 0]
    slot_iota = jnp.arange(slots, dtype=jnp.int32)
    owner_of = view // view_dev
    ahead = (owner_of[:, None] == owner_of[None, :]) & (slot_iota[None, :] < slot_iota[:, None])
    target = owner_of * cap + jnp.sum(ahead.astype(jnp.int32), axis=1)
    matches = (target[None, :] == jnp.arange(padded, dtype=jnp.int32)[:, None]).astype(F32)
    weights = node_weights(slot_pos[0, 0].astype(F32), slot_pos[1, 0].astype(F32), GRID)
    tilt_match = (tilt[:, None] == jnp.arange(tilt_dev, dtype=jnp.int32)[None, :]).astype(F32)
    chosen = exact(tilt_match, warp_grid.reshape(tilt_dev, -1))
    shift_x = jnp.sum(chosen[:, :node_count] * weights, axis=1)
    shift_y = jnp.sum(chosen[:, node_count:] * weights, axis=1)
    facts = jnp.stack(
        [
            slot_iota.astype(F32),
            ((view % view_dev) * tilt_dev + tilt).astype(F32),
            defocus[0].astype(F32),
            shift_x,
            shift_y,
        ],
        axis=1,
    )
    facts = exact(matches, facts)
    src = jnp.round(facts[:, 0]).astype(jnp.int32)
    which = jnp.round(facts[:, 1]).astype(jnp.int32)
    focus = facts[:, 2]
    shifts = facts[:, 3:5]
    meta = jnp.broadcast_to(facts[:, 2:5].T[:, :, None], (3, padded, pixels))
    first, second, nyquist = pass_tables(pixels)
    sums, extra = gather_sums(cap, src, which, own, patches[0], meta, first, second, nyquist)
    terms = exact(finish_terms(sums, extra, focus, shifts, pixels), matches)
    coef = (tilt_match.T[:, None, :] * terms[None, 1:3, :]).reshape(2 * tilt_dev, -1)
    gradient = exact(coef, weights).reshape(tilt_dev, 2 * node_count)
    new_warp = warp_step(gradient, warp_grid.reshape(tilt_dev, 2 * node_count))
    return (terms[:, None, :], new_warp.reshape(warp_grid.shape))


def solution(mesh):
    body = on_device if mesh.shape["rep"] > 1 else on_device_gathered
    in_specs = (
        P(("groups", "tilt"), "dom", None, None),
        P(("groups", "tilt"), "dom", None),
        P(("groups", "tilt"), "dom"),
        P(None, ("groups", "tilt"), "dom"),
        P(("groups", "tilt"), "dom"),
        P(("groups", "dom"), "tilt", None, "rep", None),
        P(("groups", "tilt"), None, None),
    )
    out_specs = (P(None, ("groups", "tilt"), "dom"), P(("groups", "tilt"), None, None))
    return jax.shard_map(
        body, mesh=mesh, in_specs=in_specs, out_specs=out_specs, check_vma=False
    )
```

profile of v0, /device:TPU:0, one launch (start us, length us, event | category | flops | bytes accessed | tf_op | source)
XLA Modules:
  0.0 160.3 jit_solution(6628258861343450916)
XLA Ops:
  0.6 0.3 fusion.34
  1.0 0.8 pad_maximum_fusion.second_ref
  1.8 0.7 multiply_bitcast_fusion.1
  2.5 0.1 subtract_maximum_fusion.1
  2.6 0.1 copy.25
  2.7 0.7 pad.22
  3.4 0.0 copy-start.2
  3.5 1.0 fusion.31
  4.4 0.1 fusion.2
  4.5 0.7 iota_convert_fusion.2
  5.2 0.7 bitcast_convert_fusion
  5.9 0.7 and_select_fusion.3
  6.6 0.2 convert_reduce_fusion
  6.8 0.7 multiply_add_fusion.1
  7.4 0.1 fusion.16
  7.6 0.7 compare_select_fusion.1
  8.3 0.9 broadcast_in_dim.20.meta_ref
  9.2 0.1 broadcast_multiply_fusion
  9.3 1.6 add_cosine_fusion
  10.9 1.5 fusion.waves_ref
  12.5 0.7 add_convert_fusion.pick_ref
  13.2 0.7 fusion.29.turn_ref
  13.9 0.6 broadcast_in_dim.19.unit_ref
  14.5 10.7 %fold_references.1.own_ref = bf16[40,136,128]{2,1,0:T(8,128)(2,1)} custom-call(bf16[40,2,128,128]{3,2,1,0:T(8,128)(2,1)} %bitcast.121, bf16[256,256]{1,0:T(8,128)(2,1)} %add_convert_fusion.pick_ref, bf16[128,128]{1,0:T(8,128)(2,1)} %fusion.29.turn_ref, bf16[16,128]{1,0:T(8,128)(2,1)} %broadcast_in_dim.19.unit_ref, bf16[128,512]{1,0:T(8,128)(2,1)} %fusion.waves_ref, ...), custom_call_target="tpu_custom_call" | custom-call | tf_op jit(solution)/shard_map/fold_references/pallas_call | solution.py:270
  25.2 0.0 copy-done.2
  25.2 0.2 slice_reduce_fusion.2
  25.3 0.6 broadcast_in_dim.22.nyq_ref
  25.9 0.6 fusion.4.first_ref
  26.6 111.6 %gather_sums.1 = (f32[192,8,128]{2,1,0:T(8,128)}, f32[192,8,128]{2,1,0:T(8,128)}) custom-call(s32[192]{0:T(256)} %bitcast.143, s32[192]{0:T(256)} %bitcast.142, bf16[40,136,128]{2,1,0:T(8,128)(2,1)} %fold_references.1.own_ref, bf16[128,128,128]{2,1,0:T(8,128)(2,1)} %bitcast.120, f32[3,192,128]{2,1,0:T(8,128)} %broadcast_in_dim.20.meta_ref, ...), custom_call_target="tpu_custom_call" | custom-call | tf_op jit(solution)/shard_map/gather_sums/pallas_call | solution.py:503
  138.2 0.0 copy-start
  138.2 0.0 copy-start.1
  138.2 1.4 copy.29
  139.6 0.0 copy-start.3
  139.6 1.2 slice.122
  140.9 1.3 copy.27
  142.2 0.9 fusion.10
  143.1 0.0 copy-done
  143.1 0.3 slice.126
  143.4 0.9 add_reduce_fusion
  144.3 2.0 %fusion.1 = f32[192]{0:T(256)S(1)} fusion(f32[192,8,128]{2,1,0:T(8,128)S(1)} %copy-done, f32[2,128]{1,0:T(2,128)S(1)} %add_convert_fusion.1, f32[192]{0:T(256)S(1)} %bitcast.137), kind=kLoop, calls=%fused_computation.6 | loop fusion | flops 196416 | bytes 395776 | tf_op jit(solution)/shard_map/reduce_sum | solution.py:621
  146.3 0.0 copy-done.1
  146.3 1.1 slice_reduce_fusion.1
  147.4 0.1 multiply_reduce_fusion.3
  147.6 0.1 fusion.59
  147.7 0.2 multiply_reduce_fusion.1
  147.9 0.1 multiply_reduce_fusion.2
  148.0 0.1 fusion.15
  148.2 0.0 copy-done.3
  148.2 0.2 fusion.62
  148.5 0.6 reshape.613.grad_ref
  149.1 9.3 %warp_step.1 = f32[10,512]{1,0:T(8,128)} custom-call(f32[10,512]{1,0:T(8,128)} %reshape.613.grad_ref, f32[10,512]{1,0:T(8,128)} %bitcast.129), custom_call_target="tpu_custom_call" | custom-call | tf_op jit(solution)/shard_map/warp_step/pallas_call | solution.py:553
  158.4 1.4 reshape.614
  159.7 0.6 copy.33
  (34 shorter events, 0.4 us)
Async XLA Ops:
  3.4 21.7 %copy-start.2 = (f32[2,8,2,256]{3,1,2,0:T(8,128)}, f32[2,8,2,256]{3,1,2,0:T(8,128)S(1)}, u32[]{:S(2)}) copy-start(f32[2,8,2,256]{3,1,2,0:T(8,128)S(1)} %copy.34) | copy-start | bytes 98308
  138.2 4.9 %copy-start = (f32[192,8,128]{2,1,0:T(8,128)S(1)}, f32[192,8,128]{2,1,0:T(8,128)}, u32[]{:S(2)}) copy-start(f32[192,8,128]{2,1,0:T(8,128)} %get-tuple-element.5) | copy-start | bytes 2359300
  138.2 8.1 %copy-start.1 = (f32[192,8,128]{2,1,0:T(8,128)S(1)}, f32[192,8,128]{2,1,0:T(8,128)}, u32[]{:S(2)}) copy-start(f32[192,8,128]{2,1,0:T(8,128)} %get-tuple-element.4) | copy-start | bytes 2359300
  139.6 8.5 %copy-start.3 = (s32[1,128]{1,0:T(1,128)S(1)}, s32[1,128]{1,0:T(1,128)}, u32[]{:S(2)}) copy-start(s32[1,128]{1,0:T(1,128)} %param.9) | copy-start | bytes 1540
where the time goes:
time: 161 us; the launch traced here: 160 us
  Pallas kernels  132 us (82%)
  other arithmetic  16.4 us (10%)
  local copies, waits for them, and re-layouts  9.9 us (6%)
    pallas_call x1, Pallas kernels, gather_sums(): pl.pallas_call(functools.partial(gather_kernel, chips, cap), out_shape=(j...  112 us
    pallas_call x1, Pallas kernels, fold_references(): pl.pallas_call(fold_kernel, grid=(count // group,), out_shape=jax.ShapeDt...  10.7 us
    pallas_call x1, Pallas kernels, warp_step(): pl.pallas_call(functools.partial(step_kernel, owners), out_shape=jax.Shap...  9.27 us

commit v1 on v0

v1 whole, which is shorter than its diff:
```python
import functools
import math

import jax
import jax.numpy as jnp
import numpy as np
from jax import lax
from jax.experimental import pallas as pl
from jax.experimental.pallas import tpu as pltpu
from jax.sharding import PartitionSpec as P

GRID = 16


AMPLITUDE = 0.07
TRUST_FLOOR = 0.02


def signed_freq(index, pixels):
    return jnp.where(index < pixels // 2, index, index - pixels).astype(jnp.float32)


def dft_tables(freq_rows, pixels):
    columns = jnp.arange(pixels, dtype=jnp.int32)
    table_scale = 1.0 / math.sqrt(pixels)
    turns_rows = (freq_rows[:, None] * columns[None, :] % pixels).astype(jnp.float32) * (
        2.0 * math.pi / pixels
    )
    turns_full = (columns[:, None] * columns[None, :] % pixels).astype(jnp.float32) * (
        2.0 * math.pi / pixels
    )
    row_table = jnp.concatenate([jnp.cos(turns_rows), jnp.sin(turns_rows)], axis=0) * table_scale
    col_table = jnp.concatenate([jnp.cos(turns_full), jnp.sin(turns_full)], axis=1) * table_scale
    return (row_table.astype(jnp.bfloat16), col_table.astype(jnp.bfloat16))


def node_weights(pos_x, pos_y, grid_side):
    knot_pos = jnp.arange(grid_side, dtype=jnp.int32).astype(jnp.float32)
    weight_x = jnp.maximum(0.0, 1.0 - jnp.abs(pos_x[:, None] * (grid_side - 1) - knot_pos[None, :]))
    weight_y = jnp.maximum(0.0, 1.0 - jnp.abs(pos_y[:, None] * (grid_side - 1) - knot_pos[None, :]))
    return (weight_y[:, :, None] * weight_x[:, None, :]).reshape(
        pos_x.shape[0], grid_side * grid_side
    )


def spectral_terms(spectrum, ref_blk, focus_blk, shift_blk, freq_rows, pixels):
    row_total = freq_rows.shape[0]
    v_one_cos = spectrum[:, :row_total, :pixels]
    v_one_sin = spectrum[:, :row_total, pixels:]
    v_two_cos = spectrum[:, row_total:, :pixels]
    v_two_sin = spectrum[:, row_total:, pixels:]
    real_part = v_one_cos - v_two_sin
    imag_part = -(v_one_sin + v_two_cos)
    freq_y = signed_freq(freq_rows, pixels)[None, :, None]
    freq_x = signed_freq(jnp.arange(pixels, dtype=jnp.int32), pixels)[None, None, :]
    nyquist = pixels / 2.0
    radius = (freq_y * freq_y + freq_x * freq_x) / (nyquist * nyquist)
    aberration = math.pi * focus_blk[:, None, None] * radius
    contrast = -(
        math.sqrt(1.0 - AMPLITUDE * AMPLITUDE) * jnp.sin(aberration)
        + AMPLITUDE * jnp.cos(aberration)
    )
    phase_angle = (
        2.0
        * math.pi
        / pixels
        * (freq_x * shift_blk[:, 0, None, None] + freq_y * shift_blk[:, 1, None, None])
    )
    cosine = jnp.cos(phase_angle)
    sine_part = jnp.sin(phase_angle)
    ref_real = ref_blk[:, 0].astype(jnp.float32)
    ref_imag = ref_blk[:, 1].astype(jnp.float32)
    model_real = contrast * (ref_real * cosine + ref_imag * sine_part)
    model_imag = contrast * (ref_imag * cosine - ref_real * sine_part)
    diff_real = real_part - model_real
    diff_imag = imag_part - model_imag
    inverse_area = 1.0 / (pixels * pixels)
    energy = jnp.sum(diff_real * diff_real + diff_imag * diff_imag, axis=(1, 2)) * inverse_area
    cross_term = diff_imag * model_real - diff_real * model_imag
    grad_x = 2.0 * inverse_area * jnp.sum(2.0 * math.pi / pixels * freq_x * cross_term, axis=(1, 2))
    grad_y = 2.0 * inverse_area * jnp.sum(2.0 * math.pi / pixels * freq_y * cross_term, axis=(1, 2))
    return jnp.stack([energy, grad_x, grad_y], axis=1)


def on_device(patches, slot_view, slot_tilt, slot_pos, defocus, projections, warp_grid):
    owners = lax.axis_size("dom")
    slot_count = patches.shape[1]
    pixels = patches.shape[-1]
    view_dev = projections.shape[0]
    tilt_dev = warp_grid.shape[0]
    node_count = warp_grid.shape[2]
    capacity = 3 * slot_count // (2 * owners)
    buffer_len = owners * capacity
    chosen_view = slot_view[0, :, 0]
    owner_of = chosen_view // view_dev
    owner_hits = (owner_of[:, None] == jnp.arange(owners, dtype=jnp.int32)[None, :]).astype(
        jnp.int32
    )
    earlier = jnp.cumsum(owner_hits, axis=0) - owner_hits
    slot_rank = jnp.sum(earlier * owner_hits, axis=1)
    target = owner_of * capacity + slot_rank
    matches = target[None, :] == jnp.arange(buffer_len, dtype=jnp.int32)[:, None]
    source = jnp.sum(
        jnp.where(matches, jnp.arange(slot_count, dtype=jnp.int32)[None, :], 0), axis=1
    )
    filled = jnp.any(matches, axis=1)
    patch_rows = jnp.where(filled[:, None, None], patches[0][source], jnp.zeros((), jnp.bfloat16))
    slot_meta = jnp.stack(
        [
            slot_tilt[0].astype(jnp.float32),
            (chosen_view % view_dev).astype(jnp.float32),
            defocus[0].astype(jnp.float32),
            slot_pos[0, 0].astype(jnp.float32),
            slot_pos[1, 0].astype(jnp.float32),
            jnp.ones((slot_count,), jnp.float32),
        ],
        axis=1,
    )
    meta_rows = jnp.where(filled[:, None], slot_meta[source], 0.0).astype(jnp.bfloat16)
    patch_buffer = patch_rows.reshape(owners, capacity, pixels, pixels)
    meta_buffer = meta_rows.reshape(owners, capacity, 6)
    row_span = projections.shape[3]
    freq_rows = lax.axis_index("rep") * row_span + jnp.arange(row_span, dtype=jnp.int32)
    row_table, col_table = dft_tables(freq_rows, pixels)
    row_total = freq_rows.shape[0]
    projected_flat = projections.reshape(view_dev * tilt_dev, 2, row_total, pixels)
    tilt_iota = jnp.arange(tilt_dev, dtype=jnp.int32)
    view_iota = jnp.arange(view_dev, dtype=jnp.int32)

    def one_block(inputs):
        patch_blk, index_blk, focus_blk, shift_blk = inputs
        ref_blk = projected_flat[index_blk]
        first_pass = jnp.einsum(
            "fy,byx->bfx", row_table, patch_blk, preferred_element_type=jnp.float32
        ).astype(jnp.bfloat16)
        spectrum = jnp.einsum(
            "bfx,xk->bfk", first_pass, col_table, preferred_element_type=jnp.float32
        )
        return spectral_terms(spectrum, ref_blk, focus_blk, shift_blk, freq_rows, pixels)

    patch_in = lax.all_to_all(patch_buffer, "dom", split_axis=0, concat_axis=0, tiled=True)
    meta_in = lax.all_to_all(meta_buffer, "dom", split_axis=0, concat_axis=0, tiled=True)
    senders = patch_in.shape[0]
    per_sender = patch_in.shape[1]
    slot_total = senders * per_sender
    meta_flat = meta_in.reshape(slot_total, 6).astype(jnp.float32)
    tilt_match = meta_flat[:, 0:1] == tilt_iota.astype(jnp.float32)[None, :]
    view_match = meta_flat[:, 1:2] == view_iota.astype(jnp.float32)[None, :]
    tilt_local = jnp.sum(jnp.where(tilt_match, tilt_iota[None, :], 0), axis=1)
    view_local = jnp.sum(jnp.where(view_match, view_iota[None, :], 0), axis=1)
    weights = node_weights(meta_flat[:, 3], meta_flat[:, 4], GRID)
    shifts = jnp.sum(warp_grid[tilt_local] * weights[:, None, :], axis=2)
    block_len = math.gcd(slot_total, 16)
    block_count = slot_total // block_len
    per_slot = lax.map(
        one_block,
        (
            patch_in.reshape(block_count, block_len, pixels, pixels),
            (view_local * tilt_dev + tilt_local).reshape(block_count, block_len),
            meta_flat[:, 2].reshape(block_count, block_len),
            shifts.reshape(block_count, block_len, 2),
        ),
    ).reshape(slot_total, 3)
    node_coef = (
        tilt_match.astype(jnp.float32)[:, :, None]
        * per_slot[:, None, 1:3]
        * meta_flat[:, 5, None, None]
    ).reshape(senders, per_sender, 2 * tilt_dev)
    returned = lax.all_to_all(
        per_slot.reshape(senders, per_sender, 3), "dom", split_axis=0, concat_axis=0, tiled=True
    )
    weight_all = weights.reshape(senders, per_sender, node_count)
    own_terms = returned.reshape(buffer_len, 3)[target]
    summed = lax.psum(own_terms, "rep")
    slot_terms = summed.T[:, None, :]
    gradient = jnp.dot(
        node_coef.reshape(-1, 2 * tilt_dev).T,
        weight_all.reshape(-1, node_count),
        precision=lax.Precision.HIGHEST,
        preferred_element_type=jnp.float32,
    ).reshape(tilt_dev, 2, node_count)
    whole_grad = lax.psum(gradient, ("dom", "rep"))
    new_warp = warp_grid - whole_grad / jnp.sqrt(
        whole_grad * whole_grad + TRUST_FLOOR * TRUST_FLOOR
    )
    return (slot_terms, new_warp)


CORES = 2
CHIPS = 4
EXTRA_ROWS = 8
SPEC_ROWS = 16
GUEST_CHUNKS = 4
DELTA = math.asin(AMPLITUDE)
F32 = jnp.float32
BF16 = jnp.bfloat16
OWN, NEAR, CROSS, ON_FAR, ON_OPP, NEAR_PAIR, OPP_PAIR, FAR_PAIR = range(8)


def exact(a, b, dims=(((1,), (0,)), ((), ()))):
    return lax.dot_general(
        a, b, dims, precision=lax.Precision.HIGHEST, preferred_element_type=F32
    )


def contract_last(a, b):
    return lax.dot_general(a, b, (((1,), (1,)), ((), ())), preferred_element_type=F32)


def tables(pixels):
    half = pixels // 2
    k = np.arange(pixels)
    angle = ((k[:, None] * k[None, :]) % pixels).astype(np.float32) * np.float32(
        2.0 * math.pi / pixels
    )
    scale = np.float32(1.0 / math.sqrt(pixels))
    cosine, sine = np.cos(angle) * scale, np.sin(angle) * scale
    pad = np.zeros((SPEC_ROWS - 2, pixels), np.float32)
    edge_c, edge_s = cosine[half : half + 1], sine[half : half + 1]
    first = np.concatenate(
        [cosine[:half], edge_c, edge_c, pad, sine[:half], edge_s, edge_s, pad], axis=0
    )
    second = np.concatenate(
        [np.concatenate([cosine, -sine], axis=1), np.concatenate([-sine, -cosine], axis=1)], axis=0
    )
    edge = np.zeros((SPEC_ROWS, pixels), np.float32)
    edge[2:4] = edge_c
    turn = ((k[:half, None] + k[None, :] == pixels) & (k[:half, None] > 0)).astype(np.float32)
    flip = (((k[:, None] + k[None, :]) % pixels == 0) & (k != half)[None, :]).astype(np.float32)
    unit = np.broadcast_to((k == half).astype(np.float32)[None, :], (16, pixels))
    table = np.arange(2 * pixels)
    focus = np.where(table < pixels, 1.0 + table / pixels, 2.0 + (table - pixels) / half)
    freq = np.where(k < half, k, k - pixels).astype(np.float64)
    chi = 2.0 * math.pi * focus[None, :] * (freq * freq / (half * half))[:, None]
    waves = np.concatenate([np.cos(chi), np.sin(chi)], axis=1)
    levels = np.concatenate([np.cos(chi + 2.0 * DELTA), -np.sin(chi + 2.0 * DELTA)], axis=1)
    low = [jnp.asarray(x, BF16) for x in (first, second, edge, turn, flip, unit, waves)]
    return low + [jnp.asarray(levels, F32)]


def fold_reference(pixels, real, imag, turn, flip, unit, waves, levels):
    half = pixels // 2
    lane = lax.broadcasted_iota(jnp.int32, (1, pixels), 1)
    turned = jnp.dot(turn, jnp.concatenate([real, imag], axis=1), preferred_element_type=F32)
    turned = jnp.concatenate([turned[:, :pixels], turned[:, pixels:]], axis=0).astype(BF16)
    mirror = jnp.dot(turned, flip, preferred_element_type=F32)
    r, i = real.astype(F32), imag.astype(F32)
    column = contract_last(unit, jnp.concatenate([real, imag], axis=0))[0:1]
    column = jnp.where(jnp.concatenate([lane, lane], axis=1) > half, column, 0.0)
    power = r * r + i * i
    mixed = jnp.dot(power.astype(BF16), waves, preferred_element_type=F32)
    swing = jnp.sum(mixed * levels, axis=0, keepdims=True)
    swing = swing[:, : 2 * pixels] + swing[:, 2 * pixels :]
    total = 0.5 * jnp.sum(power) - 0.5 * swing
    high = total.astype(BF16).astype(F32)
    low = total - high
    extra = jnp.concatenate(
        [
            r[half : half + 1], i[half : half + 1], column[:, :pixels], column[:, pixels:],
            high[:, :pixels], high[:, pixels:], low[:, :pixels], low[:, pixels:],
        ],
        axis=0,
    )
    return (r[:half] + mirror[:half]).astype(BF16), (i[:half] - mirror[half:]).astype(BF16), extra


def gather_kernel(cap, view_dev, chunks, view_ref, tilt_ref, pos_ref, focus_ref, warp_ref,
                  patch_hbm, proj_hbm, first_ref, second_ref, edge_ref, turn_ref, flip_ref,
                  unit_ref, waves_ref, levels_ref, terms_ref, new_ref, patch_ref, proj_ref,
                  own_ref, pair_ref, near_ref, near_pair_ref, opp_ref, opp_pair_ref, far_ref,
                  far_pair_ref, guest_ref, visit_ref, spec_ref, factor_ref, cols_ref, node_ref,
                  match_ref, sums_ref, visit_sums_ref, ints_ref, visit_ints_ref, ints_s,
                  visit_ints_s, grad_ref, held_ref, back_ref, back_in_ref, load_sem, send_sem,
                  recv_sem, guest_send, guest_recv, misc_send, misc_recv, grad_send, grad_recv):
    slots, pixels = patch_ref.shape[0], patch_ref.shape[1]
    half = pixels // 2
    refs = own_ref.shape[0]
    tilt_dev = warp_ref.shape[0]
    node_count = warp_ref.shape[2]
    per = refs // chunks
    guests = guest_ref.shape[0]
    per_guest = guests // GUEST_CHUNKS
    devices = CHIPS * CORES
    padded = devices * cap
    far_base = padded - guests
    wide = sums_ref.shape[1]
    me = lax.axis_index("dom")
    chip = me // CORES
    core = me % CORES
    partner = chip * CORES + (1 - core)
    mate_chip = chip + 1 - 2 * (chip % 2)
    mate = mate_chip * CORES + core
    cross = (CHIPS - 1 - chip) * CORES + core
    inner = (chip > 0) & (chip < CHIPS - 1)
    outer = jnp.logical_not(inner)
    barrier = pltpu.get_barrier_semaphore()
    for hop in range(1, devices):
        pl.semaphore_signal(
            barrier, inc=1, device_id={"dom": lax.rem(me + hop, devices)},
            device_id_type=pl.DeviceIdType.MESH,
        )

    def load_proj(c):
        rows = pl.ds(c * per, per)
        return pltpu.make_async_copy(proj_hbm.at[rows], proj_ref.at[rows], load_sem.at[c])

    load_patch = pltpu.make_async_copy(patch_hbm, patch_ref, load_sem.at[chunks])
    for c in range(chunks):
        load_proj(c).start()
    load_patch.start()

    def remote(src, dst, send, recv, target):
        return pltpu.make_async_remote_copy(
            src_ref=src, dst_ref=dst, send_sem=send, recv_sem=recv,
            device_id={"dom": target}, device_id_type=pl.DeviceIdType.MESH,
        )

    flows = {
        OWN: (own_ref, pair_ref, partner),
        NEAR: (own_ref, near_ref, mate),
        CROSS: (own_ref, opp_ref, cross),
        ON_FAR: (near_ref, far_ref, cross),
        ON_OPP: (opp_ref, opp_ref, mate),
        NEAR_PAIR: (near_ref, near_pair_ref, partner),
        OPP_PAIR: (opp_ref, opp_pair_ref, partner),
        FAR_PAIR: (far_ref, far_pair_ref, partner),
    }

    def flow(kind, c):
        src, dst, target = flows[kind]
        rows = pl.ds(c * per, per)
        return remote(
            src.at[rows], dst.at[rows], send_sem.at[kind, c], recv_sem.at[kind, c], target
        )

    def guest_copy(g):
        rows = pl.ds(g * per_guest, per_guest)
        return remote(
            guest_ref.at[rows], visit_ref.at[rows], guest_send.at[g], guest_recv.at[g], mate
        )

    ints_copy = remote(ints_ref, visit_ints_ref, misc_send.at[0], misc_recv.at[0], mate)
    back_copy = remote(back_ref, back_in_ref, misc_send.at[1], misc_recv.at[1], mate)

    def fold(c):
        load_proj(c).wait()

        def one(i, carry):
            n = c * per + i
            top, bottom, extra = fold_reference(
                pixels, proj_ref[n, 0], proj_ref[n, 1], turn_ref[...], flip_ref[...],
                unit_ref[...], waves_ref[...], levels_ref[...],
            )
            own_ref[n, :half] = top
            own_ref[n, half:pixels] = bottom
            own_ref[n, pixels:] = extra.astype(BF16)
            return carry

        lax.fori_loop(0, per, one, 0, unroll=2)

    def send_own(c):
        flow(NEAR, c).start()

        @pl.when(inner)
        def _():
            flow(CROSS, c).start()

        flow(OWN, c).start()

    lane = lax.broadcasted_iota(jnp.int32, (1, pixels), 1)
    line = jnp.where(lane < half, lane, lane - pixels).astype(F32)
    lane_f = lane.astype(F32)

    def route():
        chip_f, core_f, mate_f = chip.astype(F32), core.astype(F32), mate_chip.astype(F32)
        opp_f = (CHIPS - 1) - jnp.where(inner, chip_f, mate_f)
        view = view_ref[...].astype(F32)
        owner = jnp.floor((view + 0.5) * (1.0 / view_dev))
        owner_chip = jnp.floor((owner + 0.5) * (1.0 / CORES))
        owner_core = owner - CORES * owner_chip
        role = jnp.where(
            owner_chip == chip_f, 0.0,
            jnp.where(owner_chip == mate_f, 1.0, jnp.where(owner_chip == opp_f, 2.0, 3.0)),
        )
        key = role * CORES + jnp.where(owner_core == core_f, 0.0, 1.0)
        tilt = tilt_ref[...].astype(F32)
        which = (view - owner * view_dev) * tilt_dev + tilt
        pos = pos_ref[...].astype(F32)
        block = jnp.concatenate(
            [key, which, pos, focus_ref[...].astype(F32), tilt,
             jnp.zeros((slots - 6, slots), F32)],
            axis=0,
        )
        cols = block.T
        cols_ref[...] = cols
        row = lax.broadcasted_iota(jnp.int32, (slots, slots), 0)
        col = lax.broadcasted_iota(jnp.int32, (slots, slots), 1)
        ahead = jnp.where((cols[:, 0:1] == key) & (col < row), 1.0, 0.0)
        target = cols[:, 0:1] * cap + jnp.sum(ahead, axis=1, keepdims=True)
        place = lax.broadcasted_iota(jnp.int32, (1, wide), 1).astype(F32)
        match = jnp.where(target == place, 1.0, 0.0)
        match_ref[...] = match
        slot = lax.broadcasted_iota(jnp.int32, (slots, wide), 0).astype(F32)
        source = jnp.sum(match * slot, axis=0, keepdims=True)
        chosen = jnp.sum(match * cols[:, 1:2], axis=0, keepdims=True)
        ints = jnp.concatenate([source, chosen, jnp.zeros((6, wide), F32)], axis=0)
        ints_ref[...] = (ints + 0.5).astype(jnp.int32)

    def place_nodes():
        node = lax.broadcasted_iota(jnp.int32, (1, node_count), 1).astype(F32)
        node_y = jnp.floor((node + 0.5) * (1.0 / GRID))
        node_x = node - node_y * GRID
        weight_x = jnp.maximum(0.0, 1.0 - jnp.abs(cols_ref[:, 2:3] * (GRID - 1) - node_x))
        weight_y = jnp.maximum(0.0, 1.0 - jnp.abs(cols_ref[:, 3:4] * (GRID - 1) - node_y))
        weights = weight_y * weight_x
        node_ref[...] = weights
        hits = jnp.where(cols_ref[:, 5:6] == lane_f[:, :16], 1.0, 0.0)
        spare = jnp.zeros((16 - tilt_dev, node_count), F32)
        for axis in range(2):
            grid = jnp.concatenate([warp_ref[:, axis, :], spare], axis=0)
            shift = jnp.sum(exact(hits, grid) * weights, axis=1, keepdims=True)
            cols_ref[:, 6 + axis : 7 + axis] = shift

    step_angle = 2.0 * math.pi / pixels
    norm = 1.0 / (half * half)
    block_slots = 16

    def factors(block, carry):
        rows = pl.ds(pl.multiple_of(block * block_slots, block_slots), block_slots)
        cols = cols_ref[rows]
        focus, shift_x, shift_y = cols[:, 4:5], cols[:, 6:7], cols[:, 7:8]
        chi = math.pi * focus * (line * line * norm)
        phi_x = step_angle * shift_x * line
        phi_y = step_angle * shift_y * line
        c_x, s_x = jnp.cos(chi), jnp.sin(chi)
        s_y = s_x * math.cos(DELTA) + c_x * math.sin(DELTA)
        c_y = c_x * math.cos(DELTA) - s_x * math.sin(DELTA)
        p_x, q_x, p_y, q_y = jnp.cos(phi_x), jnp.sin(phi_x), jnp.cos(phi_y), jnp.sin(phi_y)
        tall = (s_y * p_y, s_y * q_y, c_y * p_y, c_y * q_y)
        a, b, c, d = c_x * p_x, c_x * q_x, s_x * p_x, s_x * q_x
        e, f, g, h = (v[:, half : half + 1] for v in (a, b, c, d))
        edge_re = -(tall[0] * e - tall[1] * f + tall[2] * g - tall[3] * h)
        edge_im = -(tall[0] * f + tall[1] * e + tall[2] * h + tall[3] * g)
        tall = tuple(jnp.where(lane == half + 1, pltpu.roll(v, 1, 1), v) for v in tall)
        place = jnp.where(focus < 2.0, (focus - 1.0) * pixels, pixels + (focus - 2.0) * half)
        hit_low = jnp.where(place == lane_f, -0.5, 0.0)
        hit_high = jnp.where(place == lane_f + pixels, -0.5, 0.0)
        zero = jnp.zeros_like(a)
        values = tall + (a, b, c, d, edge_re, edge_im, zero, zero,
                         hit_low, hit_high, hit_low, hit_high)
        for index, value in enumerate(values):
            factor_ref[rows, index] = value
        return carry

    row8 = lax.broadcasted_iota(jnp.int32, (8, pixels), 0)
    main_rows = half + SPEC_ROWS

    def spectra(indices, put):
        count = len(indices)
        blocks = [patch_ref[s] for s in indices]
        wides = []
        for n in range(0, count, 2):
            both = jnp.concatenate(blocks[n : n + 2], axis=1)
            v = jnp.dot(first_ref[...], both, preferred_element_type=F32)
            edge = contract_last(edge_ref[...], jnp.concatenate(blocks[n : n + 2], axis=0))
            for part in range(2):
                at = slice(part * pixels, (part + 1) * pixels)
                one = jnp.concatenate([v[:half, at], v[half:main_rows, at] + edge[:, at]], axis=0)
                wides.append(
                    jnp.concatenate([one.astype(BF16), v[main_rows:, at].astype(BF16)], axis=1)
                )
        spectrum = jnp.dot(
            jnp.concatenate(wides, axis=0), second_ref[...], preferred_element_type=F32
        )
        for n in range(count):
            factor = factor_ref[indices[n]]
            tall = factor[0:4]
            a, b, c, d = factor[4:5], factor[5:6], factor[6:7], factor[7:8]
            rows = jnp.concatenate(
                [
                    jnp.concatenate([-a, b, -c, d], axis=0),
                    jnp.concatenate([-b, -a, -d, -c], axis=0),
                ],
                axis=1,
            )
            tall_high = tall.astype(BF16).astype(F32)
            row_high = rows.astype(BF16).astype(F32)
            tall_low, row_low = tall - tall_high, rows - row_high
            tall_all = jnp.concatenate(
                [tall_high, tall_high, tall_low, jnp.zeros_like(tall_low)], axis=0
            ).astype(BF16)
            row_all = jnp.concatenate(
                [row_high, row_low, row_high, jnp.zeros_like(row_low)], axis=0
            ).astype(BF16)
            turn = lax.dot_general(
                tall_all, row_all, (((0,), (0,)), ((), ())), preferred_element_type=F32
            )
            base = n * main_rows
            x_re = spectrum[base : base + half, :pixels]
            x_im = spectrum[base : base + half, pixels:]
            t_re, t_im = turn[:half, :pixels], turn[:half, pixels:]
            put(n, slice(0, half), x_re * t_re - x_im * t_im)
            put(n, slice(half, pixels), x_re * t_im + x_im * t_re)
            power = x_re * x_re + x_im * x_im
            power = jnp.sum(power.reshape(half // 8, 8, pixels), axis=0) * 2.0 - jnp.where(
                row8 == 0, power[:8], 0.0
            )
            x_re = spectrum[base + half : base + half + 8, :pixels]
            x_im = spectrum[base + half : base + half + 8, pixels:]
            power = power + jnp.where(row8 == 0, x_re * x_re + x_im * x_im, 0.0)
            edge_turn = (row8 == 2) | (row8 == 3)
            t_re = jnp.where(edge_turn, factor[8:9], turn[half : half + 8, :pixels])
            t_im = jnp.where(edge_turn, factor[9:10], turn[half : half + 8, pixels:])
            y_re = x_re * t_re - x_im * t_im
            y_im = x_re * t_im + x_im * t_re
            odd = row8 % 2 == 1
            straight = jnp.where(odd, y_im, y_re)
            crossed = jnp.where(odd, -y_re, y_im)
            straight = jnp.where(row8 < 4, straight, factor[8:16])
            power = jnp.sum(power, axis=0, keepdims=True)
            high = power.astype(BF16).astype(F32)
            crossed = jnp.where(
                row8 < 4, crossed,
                jnp.where(row8 == 4, high, jnp.where(row8 == 5, power - high, 0.0)),
            )
            put(n, slice(pixels, pixels + 16), jnp.concatenate([straight, crossed], axis=0))

    weight_x = jnp.where(row8 < 2, line, jnp.where(row8 < 4, -float(half), 0.0))
    weight_y = jnp.where(row8 < 2, -float(half), jnp.where(row8 < 4, line, 0.0))
    freq_y = lax.broadcasted_iota(jnp.int32, (half, pixels), 0).astype(F32)

    def stack(x):
        return jnp.sum(x.reshape(half // 8, 8, pixels), axis=0)

    def meet(y, ref, out_ref, place):
        y = y.astype(F32)
        r = ref.astype(F32)
        y_re, y_im, straight = y[:half], y[half:pixels], y[pixels : pixels + 8]
        crossed = y[pixels + 8 :]
        r_re, r_im, extra = r[:half], r[half:pixels], r[pixels:]
        match = stack(y_re * r_re + y_im * r_im) + straight * extra
        swirl = y_im * r_re - y_re * r_im
        edge = crossed * extra
        energy = jnp.where((row8 == 4) | (row8 == 5), crossed, 0.0) - 2.0 * match
        grad_x = stack(swirl) * line + edge * weight_x
        grad_y = stack(swirl * freq_y) + edge * weight_y
        for index, value in enumerate((energy, grad_x, grad_y)):
            out_ref[index, pl.ds(place, 1)] = jnp.sum(value, axis=0, keepdims=True)

    def slot_at(p):
        return jnp.clip(ints_s[0, p], 0, slots - 1)

    def ref_at(held, p):
        return jnp.clip(held[1, p], 0, refs - 1)

    def process(refs_ref, role):
        def some(step, carry):
            for u in range(4):
                p = role * cap + step * 4 + u
                meet(spec_ref[slot_at(p)], refs_ref[ref_at(ints_s, p)], sums_ref, p)
            return carry

        lax.fori_loop(0, cap // 4, some, 0)

    def entertain(refs_ref, part):
        def some(step, carry):
            for u in range(4):
                g = part * cap + step * 4 + u
                p = far_base + g
                place = p - (wide - pixels)
                meet(visit_ref[g], refs_ref[ref_at(visit_ints_s, p)], visit_sums_ref, place)
            return carry

        lax.fori_loop(0, cap // 4, some, 0)

    def transform(low, high):
        def some(step, carry):
            base = low + step * 4

            def put(n, rows, value):
                spec_ref[base + n, rows] = value

            spectra([base + n for n in range(4)], put)
            return carry

        lax.fori_loop(0, (high - low) // 4, some, 0)

    def transform_guests(low, high):
        def some(step, carry):
            base = low + step * 4

            def put(n, rows, value):
                guest_ref[base + n, rows] = value.astype(BF16)

            spectra([slot_at(far_base + base + n) for n in range(4)], put)
            return carry

        lax.fori_loop(0, (high - low) // 4, some, 0)

    fold(0)
    pl.semaphore_wait(barrier, devices - 1)
    route()
    send_own(0)
    for c in range(1, chunks):
        fold(c)
        if c > 1:
            send_own(c - 1)
    ints_load = pltpu.make_async_copy(ints_ref, ints_s, load_sem.at[chunks + 1])
    ints_load.start()

    @pl.when(outer)
    def _():
        ints_copy.start()

    sums_ref[...] = jnp.zeros_like(sums_ref)
    visit_sums_ref[...] = jnp.zeros_like(visit_sums_ref)
    place_nodes()
    if chunks > 1:
        send_own(chunks - 1)
    lax.fori_loop(0, slots // block_slots, factors, 0)
    load_patch.wait()
    ints_load.wait()

    @pl.when(outer)
    def _():
        for g in range(GUEST_CHUNKS):
            transform_guests(g * per_guest, (g + 1) * per_guest)
            if g > 0:
                guest_copy(g - 1).start()

    def pass_on(c):
        flow(NEAR, c).wait_recv()

        @pl.when(inner)
        def _():
            flow(ON_FAR, c).start()
            flow(CROSS, c).wait_recv()
            flow(ON_OPP, c).start()
            flow(OPP_PAIR, c).start()

        flow(NEAR_PAIR, c).start()

    segments = 4
    seg = slots // segments
    done = 0
    for n in range(segments):
        transform(n * seg, (n + 1) * seg)
        if n == 0:
            @pl.when(outer)
            def _():
                guest_copy(GUEST_CHUNKS - 1).start()
        upto = chunks * (n + 1) // segments
        while done < upto:
            pass_on(done)
            done += 1

    process(own_ref, 0)
    for c in range(chunks):
        flow(OWN, c).wait_recv()
    process(pair_ref, 1)
    process(near_ref, 2)
    for c in range(chunks):
        flow(NEAR_PAIR, c).wait_recv()
    process(near_pair_ref, 3)

    @pl.when(outer)
    def _():
        for c in range(chunks):
            flow(ON_OPP, c).wait_recv()
            flow(OPP_PAIR, c).start()

    process(opp_ref, 4)
    for c in range(chunks):
        flow(OPP_PAIR, c).wait_recv()
    process(opp_pair_ref, 5)

    visit_load = pltpu.make_async_copy(visit_ints_ref, visit_ints_s, load_sem.at[chunks + 2])
    ones = jnp.ones((8, pixels), F32)

    @pl.when(inner)
    def _():
        ints_copy.wait_recv()
        visit_load.start()
        visit_load.wait()
        for c in range(chunks):
            flow(ON_FAR, c).wait_recv()
            flow(FAR_PAIR, c).start()
        process(far_ref, 6)
        for c in range(chunks):
            flow(FAR_PAIR, c).wait_recv()
        process(far_pair_ref, 7)
        for g in range(GUEST_CHUNKS):
            guest_copy(g).wait_recv()
        entertain(far_ref, 0)
        entertain(far_pair_ref, 1)
        parts = [exact(ones, visit_sums_ref[k], (((1,), (1,)), ((), ()))) for k in range(3)]
        back_ref[...] = jnp.where(row8 == 0, parts[0], jnp.where(row8 == 1, parts[1], parts[2]))
        back_copy.start()

    parts = [exact(ones, sums_ref[k], (((1,), (1,)), ((), ()))) for k in range(3)]
    row_wide = lax.broadcasted_iota(jnp.int32, (8, wide), 0)
    mixed = jnp.where(row_wide == 0, parts[0], jnp.where(row_wide == 1, parts[1], parts[2]))
    cols_ref[:8, :] = jnp.zeros((8, slots), F32)

    @pl.when(outer)
    def _():
        back_copy.wait_recv()
        cols_ref[:8, :] = back_in_ref[...]

    mixed = jnp.concatenate(
        [mixed[:, : wide - pixels], mixed[:, wide - pixels :] + cols_ref[:8, :]], axis=1
    )
    area = 1.0 / (pixels * pixels)
    mixed = mixed * jnp.where(row_wide == 0, area, 2.0 * area * step_angle)
    terms = exact(mixed, match_ref[...], (((1,), (1,)), ((), ())))
    terms_ref[...] = terms[:3]
    row16 = lax.broadcasted_iota(jnp.int32, (16, slots), 0)
    on_tilt = row16 == tilt_ref[...]
    for axis in range(2):
        coef = jnp.where(on_tilt, terms[1 + axis : 2 + axis], 0.0)
        grad = exact(coef, node_ref[...])
        grad_ref[:, axis * node_count : (axis + 1) * node_count] = grad[:tilt_dev]

    def grad_copy(hop):
        return remote(
            grad_ref, held_ref.at[hop - 1], grad_send.at[hop - 1], grad_recv.at[hop - 1],
            lax.rem(me + hop, devices),
        )

    for hop in range(1, devices):
        grad_copy(hop).start()
    for c in range(chunks):
        flow(OWN, c).wait_send()
        flow(NEAR, c).wait_send()
        flow(NEAR_PAIR, c).wait_send()
        flow(OPP_PAIR, c).wait_send()

    @pl.when(inner)
    def _():
        for c in range(chunks):
            flow(CROSS, c).wait_send()
            flow(ON_FAR, c).wait_send()
            flow(ON_OPP, c).wait_send()
            flow(FAR_PAIR, c).wait_send()
        back_copy.wait_send()

    @pl.when(outer)
    def _():
        ints_copy.wait_send()
        for g in range(GUEST_CHUNKS):
            guest_copy(g).wait_send()

    for hop in range(1, devices):
        grad_copy(hop).wait()
    total = grad_ref[...]
    for hop in range(1, devices):
        total = total + held_ref[hop - 1]
    change = total / jnp.sqrt(total * total + TRUST_FLOOR * TRUST_FLOOR)
    for axis in range(2):
        at = slice(axis * node_count, (axis + 1) * node_count)
        new_ref[:, axis, :] = warp_ref[:, axis, :] - change[:, at]


def on_device_gathered(
    patches, slot_view, slot_tilt, slot_pos, defocus, projections, warp_grid
):
    pixels = patches.shape[-1]
    slots = patches.shape[1]
    view_dev = projections.shape[0]
    tilt_dev = warp_grid.shape[0]
    node_count = warp_grid.shape[2]
    devices = CHIPS * CORES
    cap = 3 * slots // (2 * devices)
    refs = view_dev * tilt_dev
    chunks = math.gcd(refs, 5)
    guests = CORES * cap
    wide = 2 * pixels
    rows = pixels + EXTRA_ROWS
    spec_rows = pixels + 2 * EXTRA_ROWS
    vmem = pl.BlockSpec(memory_space=pltpu.VMEM)
    anywhere = pl.BlockSpec(memory_space=pl.ANY)
    dma = pltpu.SemaphoreType.DMA
    block = pltpu.VMEM((refs, rows, pixels), BF16)
    scratch = [
        pltpu.VMEM((slots, pixels, pixels), BF16),
        pltpu.VMEM((refs, 2, pixels, pixels), BF16),
    ] + [block] * 8 + [
        pltpu.VMEM((guests, spec_rows, pixels), BF16),
        pltpu.VMEM((guests, spec_rows, pixels), BF16),
        pltpu.VMEM((slots, spec_rows, pixels), F32),
        pltpu.VMEM((slots, 16, pixels), F32),
        pltpu.VMEM((slots, slots), F32),
        pltpu.VMEM((slots, node_count), F32),
        pltpu.VMEM((slots, wide), F32),
        pltpu.VMEM((3, wide, pixels), F32),
        pltpu.VMEM((3, pixels, pixels), F32),
        pltpu.VMEM((8, wide), jnp.int32),
        pltpu.VMEM((8, wide), jnp.int32),
        pltpu.SMEM((8, wide), jnp.int32),
        pltpu.SMEM((8, wide), jnp.int32),
        pltpu.VMEM((tilt_dev, 2 * node_count), F32),
        pltpu.VMEM((devices - 1, tilt_dev, 2 * node_count), F32),
        pltpu.VMEM((8, pixels), F32),
        pltpu.VMEM((8, pixels), F32),
        dma((chunks + 3,)),
        dma((8, chunks)),
        dma((8, chunks)),
        dma((GUEST_CHUNKS,)),
        dma((GUEST_CHUNKS,)),
        dma((2,)),
        dma((2,)),
        dma((devices - 1,)),
        dma((devices - 1,)),
    ]
    terms, new_warp = pl.pallas_call(
        functools.partial(gather_kernel, cap, view_dev, chunks),
        out_shape=(
            jax.ShapeDtypeStruct((3, slots), F32),
            jax.ShapeDtypeStruct(warp_grid.shape, F32),
        ),
        in_specs=[vmem] * 5 + [anywhere] * 2 + [vmem] * 8,
        out_specs=(vmem, vmem),
        scratch_shapes=scratch,
        compiler_params=pltpu.CompilerParams(
            collective_id=0, has_side_effects=True, vmem_limit_bytes=56 * 1024 * 1024
        ),
        name="gather_sums",
    )(
        slot_view.reshape(1, slots), slot_tilt, slot_pos.reshape(2, slots), defocus, warp_grid,
        patches[0], projections.reshape(refs, 2, pixels, pixels), *tables(pixels),
    )
    return (terms[:, None, :], new_warp)


def solution(mesh):
    on_chips = mesh.shape["rep"] == 1 and mesh.shape["dom"] == CHIPS * CORES
    body = on_device_gathered if on_chips else on_device
    in_specs = (
        P(("groups", "tilt"), "dom", None, None),
        P(("groups", "tilt"), "dom", None),
        P(("groups", "tilt"), "dom"),
        P(None, ("groups", "tilt"), "dom"),
        P(("groups", "tilt"), "dom"),
        P(("groups", "dom"), "tilt", None, "rep", None),
        P(("groups", "tilt"), None, None),
    )
    out_specs = (P(None, ("groups", "tilt"), "dom"), P(("groups", "tilt"), None, None))
    return jax.shard_map(
        body, mesh=mesh, in_specs=in_specs, out_specs=out_specs, check_vma=False
    )
```

time: 161 us -> 91.2 us (0.57)
  Pallas kernels: 132 us -> 87.8 us
  other arithmetic: 16.4 us -> 0 us
  local copies, waits for them, and re-layouts: 9.9 us -> 2.57 us
    pallas_call x3 -> x1, Pallas kernels: 132 us -> 87.8 us  [on_device_gathered(): pl.pallas_call(functools.partial(gather_kernel, cap, view_dev, chunks), o...]
    reduce_sum x10 -> x0, other arithmetic: 5.71 us -> none  [the longest x1 1.97 us: finish_terms(): model_power = jnp.sum(jnp.where(hit, table_high + table_low, 0.0), axis=1)]
    convert_element_type x13 -> x0, other arithmetic: 4.9 us -> none  [the longest x1 1.49 us: fold_references(): tables = (picks, turn, unit, waves.astype(BF16), weights)]
    pallas_call x2 -> x0, local copies, waits for them, and re-layouts: 2.69 us -> none  [gather_sums(): pl.pallas_call(functools.partial(gather_kernel, chips, cap), out_shape=(j...]
    broadcast_in_dim x3 -> x0, local copies, waits for them, and re-layouts: 2.08 us -> none  [the longest x1 0.88 us: on_device_gathered(): meta = jnp.broadcast_to(facts[:, 2:5].T[:, :, None], (3, padded, pixels))]
    reshape x2 -> x0, local copies, waits for them, and re-layouts: 1.99 us -> none  [the longest x1 1.38 us: on_device_gathered(): return (terms[:, None, :], new_warp.reshape(warp_grid.shape))]
    slice x4 -> x0, local copies, waits for them, and re-layouts: 1.67 us -> none  [the longest x1 1.22 us: finish_terms(): extra[:, 1]]
where the time goes in v1:
time: 91.2 us; the launch traced here: 91 us
  Pallas kernels  87.8 us (96%)
  local copies, waits for them, and re-layouts  2.57 us (3%)
    pallas_call x1, Pallas kernels, on_device_gathered(): pl.pallas_call(functools.partial(gather_kernel, cap, view_dev, chunks), o...  87.8 us
    unnamed x2, local copies, waits for them, and re-layouts  2.57 us

profile of v1, /device:TPU:0, one launch (start us, length us, event | category | flops | bytes accessed | tf_op | source)
XLA Modules:
  0.0 91.0 jit_solution(6842957555177596757)
XLA Ops:
  0.6 87.8 %gather_sums.1 = (f32[3,128]{1,0:T(4,128)}, f32[10,2,256]{2,1,0:T(2,128)}) custom-call(s32[1,128]{1,0:T(1,128)} %bitcast.8, s32[1,128]{1,0:T(1,128)} %tilt_ref.1, bf16[2,128]{1,0:T(2,128)(2,1)} %bitcast.9, bf16[1,128]{1,0:T(2,128)(2,1)} %focus_ref.1, f32[10,2,256]{2,1,0:T(2,128)} %warp_ref.1, bf16[128,128,128]{2,1,0:T(8,128)(2,1)} %bitcast.5, ...), custom_call_target="tpu_custom_call" | custom-call | tf_op jit(solution)/shard_map/gather_sums/pallas_call | solution.py:815
  88.4 1.2 %copy.17 = f32[3,1,128]{2,1,0:T(1,128)} copy(f32[3,1,128]{2,0,1:T(4,128)} %bitcast.7) | data formatting | bytes 3072
  89.6 1.3 %copy.19 = f32[10,2,256]{2,1,0:T(2,128)} copy(f32[10,2,256]{2,1,0:T(2,128)} %get-tuple-element.11) | data formatting | bytes 40960

commit v2 on v1

--- a/solution.py
+++ b/solution.py
@@ -190,7 +190,6 @@
 CHIPS = 4
 EXTRA_ROWS = 8
 SPEC_ROWS = 16
-GUEST_CHUNKS = 4
 DELTA = math.asin(AMPLITUDE)
 F32 = jnp.float32
 BF16 = jnp.bfloat16
@@ -264,26 +263,30 @@
     return (r[:half] + mirror[:half]).astype(BF16), (i[:half] - mirror[half:]).astype(BF16), extra
 
 
-def gather_kernel(cap, view_dev, chunks, view_ref, tilt_ref, pos_ref, focus_ref, warp_ref,
-                  patch_hbm, proj_hbm, first_ref, second_ref, edge_ref, turn_ref, flip_ref,
-                  unit_ref, waves_ref, levels_ref, terms_ref, new_ref, patch_ref, proj_ref,
-                  own_ref, pair_ref, near_ref, near_pair_ref, opp_ref, opp_pair_ref, far_ref,
-                  far_pair_ref, guest_ref, visit_ref, spec_ref, factor_ref, cols_ref, node_ref,
-                  match_ref, sums_ref, visit_sums_ref, ints_ref, visit_ints_ref, ints_s,
-                  visit_ints_s, grad_ref, held_ref, back_ref, back_in_ref, load_sem, send_sem,
-                  recv_sem, guest_send, guest_recv, misc_send, misc_recv, grad_send, grad_recv):
+def gather_kernel(cap, view_dev, bounds, guest_bounds, view_ref, tilt_ref, pos_ref, focus_ref,
+                  warp_ref, patch_hbm, proj_hbm, first_hbm, second_hbm, edge_hbm, turn_hbm,
+                  flip_hbm, unit_hbm, waves_hbm, levels_hbm, terms_ref, new_ref, first_ref,
+                  second_ref, edge_ref, turn_ref, flip_ref, unit_ref, waves_ref, levels_ref,
+                  patch_ref, proj_ref, own_ref, pair_ref, near_ref, near_pair_ref, opp_ref,
+                  opp_pair_ref, far_ref, far_pair_ref, guest_ref, visit_ref, spec_ref,
+                  visit_spec_ref, factor_ref, visit_factor_ref, cols_ref, visit_cols_ref,
+                  node_ref, visit_node_ref, match_ref, sums_ref, visit_sums_ref, ints_ref,
+                  visit_ints_ref, ints_s, visit_ints_s, meta_ref, visit_meta_ref, grad_ref,
+                  held_ref, back_ref, back_in_ref, load_sem, table_sem, send_sem, recv_sem,
+                  guest_send, guest_recv, misc_send, misc_recv, grad_send, grad_recv):
     slots, pixels = patch_ref.shape[0], patch_ref.shape[1]
     half = pixels // 2
     refs = own_ref.shape[0]
     tilt_dev = warp_ref.shape[0]
     node_count = warp_ref.shape[2]
-    per = refs // chunks
+    chunks = len(bounds) - 1
     guests = guest_ref.shape[0]
-    per_guest = guests // GUEST_CHUNKS
+    guest_chunks = len(guest_bounds) - 1
     devices = CHIPS * CORES
     padded = devices * cap
     far_base = padded - guests
     wide = sums_ref.shape[1]
+    shift_lanes = wide - pixels
     me = lax.axis_index("dom")
     chip = me // CORES
     core = me % CORES
@@ -294,18 +297,34 @@
     inner = (chip > 0) & (chip < CHIPS - 1)
     outer = jnp.logical_not(inner)
     barrier = pltpu.get_barrier_semaphore()
-    for hop in range(1, devices):
+
+    def greet(device):
         pl.semaphore_signal(
-            barrier, inc=1, device_id={"dom": lax.rem(me + hop, devices)},
-            device_id_type=pl.DeviceIdType.MESH,
-        )
+            barrier, inc=1, device_id={"dom": device}, device_id_type=pl.DeviceIdType.MESH
+        )
+
+    greet(mate)
+    greet(partner)
+
+    @pl.when(inner)
+    def _():
+        greet(cross)
 
     def load_proj(c):
-        rows = pl.ds(c * per, per)
+        rows = pl.ds(bounds[c], bounds[c + 1] - bounds[c])
         return pltpu.make_async_copy(proj_hbm.at[rows], proj_ref.at[rows], load_sem.at[c])
 
     load_patch = pltpu.make_async_copy(patch_hbm, patch_ref, load_sem.at[chunks])
-    for c in range(chunks):
+    sources = (turn_hbm, flip_hbm, unit_hbm, waves_hbm, levels_hbm, first_hbm, second_hbm, edge_hbm)
+    targets = (turn_ref, flip_ref, unit_ref, waves_ref, levels_ref, first_ref, second_ref, edge_ref)
+    load_tables = [
+        pltpu.make_async_copy(a, b, table_sem.at[n]) for n, (a, b) in enumerate(zip(sources, targets))
+    ]
+    fold_tables = 5
+    load_proj(0).start()
+    for load in load_tables:
+        load.start()
+    for c in range(1, chunks):
         load_proj(c).start()
     load_patch.start()
 
@@ -328,25 +347,25 @@
 
     def flow(kind, c):
         src, dst, target = flows[kind]
-        rows = pl.ds(c * per, per)
+        rows = pl.ds(bounds[c], bounds[c + 1] - bounds[c])
         return remote(
             src.at[rows], dst.at[rows], send_sem.at[kind, c], recv_sem.at[kind, c], target
         )
 
     def guest_copy(g):
-        rows = pl.ds(g * per_guest, per_guest)
+        rows = pl.ds(guest_bounds[g], guest_bounds[g + 1] - guest_bounds[g])
         return remote(
             guest_ref.at[rows], visit_ref.at[rows], guest_send.at[g], guest_recv.at[g], mate
         )
 
-    ints_copy = remote(ints_ref, visit_ints_ref, misc_send.at[0], misc_recv.at[0], mate)
+    meta_copy = remote(meta_ref, visit_meta_ref, misc_send.at[0], misc_recv.at[0], mate)
     back_copy = remote(back_ref, back_in_ref, misc_send.at[1], misc_recv.at[1], mate)
 
     def fold(c):
         load_proj(c).wait()
 
         def one(i, carry):
-            n = c * per + i
+            n = bounds[c] + i
             top, bottom, extra = fold_reference(
                 pixels, proj_ref[n, 0], proj_ref[n, 1], turn_ref[...], flip_ref[...],
                 unit_ref[...], waves_ref[...], levels_ref[...],
@@ -356,7 +375,7 @@
             own_ref[n, pixels:] = extra.astype(BF16)
             return carry
 
-        lax.fori_loop(0, per, one, 0, unroll=2)
+        lax.fori_loop(0, bounds[c + 1] - bounds[c], one, 0, unroll=2)
 
     def send_own(c):
         flow(NEAR, c).start()
@@ -406,13 +425,16 @@
         ints = jnp.concatenate([source, chosen, jnp.zeros((6, wide), F32)], axis=0)
         ints_ref[...] = (ints + 0.5).astype(jnp.int32)
 
-    def place_nodes():
+    def node_weights_of(cols):
         node = lax.broadcasted_iota(jnp.int32, (1, node_count), 1).astype(F32)
         node_y = jnp.floor((node + 0.5) * (1.0 / GRID))
         node_x = node - node_y * GRID
-        weight_x = jnp.maximum(0.0, 1.0 - jnp.abs(cols_ref[:, 2:3] * (GRID - 1) - node_x))
-        weight_y = jnp.maximum(0.0, 1.0 - jnp.abs(cols_ref[:, 3:4] * (GRID - 1) - node_y))
-        weights = weight_y * weight_x
+        weight_x = jnp.maximum(0.0, 1.0 - jnp.abs(cols[:, 2:3] * (GRID - 1) - node_x))
+        weight_y = jnp.maximum(0.0, 1.0 - jnp.abs(cols[:, 3:4] * (GRID - 1) - node_y))
+        return weight_y * weight_x
+
+    def place_nodes():
+        weights = node_weights_of(cols_ref)
         node_ref[...] = weights
         hits = jnp.where(cols_ref[:, 5:6] == lane_f[:, :16], 1.0, 0.0)
         spare = jnp.zeros((16 - tilt_dev, node_count), F32)
@@ -420,12 +442,13 @@
             grid = jnp.concatenate([warp_ref[:, axis, :], spare], axis=0)
             shift = jnp.sum(exact(hits, grid) * weights, axis=1, keepdims=True)
             cols_ref[:, 6 + axis : 7 + axis] = shift
+        meta_ref[...] = exact(cols_ref[...].T[:8], match_ref[...])
 
     step_angle = 2.0 * math.pi / pixels
     norm = 1.0 / (half * half)
     block_slots = 16
 
-    def factors(block, carry):
+    def factors(cols_ref, factor_ref, block, carry):
         rows = pl.ds(pl.multiple_of(block * block_slots, block_slots), block_slots)
         cols = cols_ref[rows]
         focus, shift_x, shift_y = cols[:, 4:5], cols[:, 6:7], cols[:, 7:8]
@@ -455,9 +478,8 @@
     row8 = lax.broadcasted_iota(jnp.int32, (8, pixels), 0)
     main_rows = half + SPEC_ROWS
 
-    def spectra(indices, put):
-        count = len(indices)
-        blocks = [patch_ref[s] for s in indices]
+    def spectra(blocks, factor_blocks, put):
+        count = len(blocks)
         wides = []
         for n in range(0, count, 2):
             both = jnp.concatenate(blocks[n : n + 2], axis=1)
@@ -473,7 +495,7 @@
             jnp.concatenate(wides, axis=0), second_ref[...], preferred_element_type=F32
         )
         for n in range(count):
-            factor = factor_ref[indices[n]]
+            factor = factor_blocks[n]
             tall = factor[0:4]
             a, b, c, d = factor[4:5], factor[5:6], factor[6:7], factor[7:8]
             rows = jnp.concatenate(
@@ -562,16 +584,19 @@
 
         lax.fori_loop(0, cap // 4, some, 0)
 
-    def entertain(refs_ref, part):
-        def some(step, carry):
+    def entertain(low, high):
+        def some(refs_ref, step, carry):
             for u in range(4):
-                g = part * cap + step * 4 + u
+                g = step * 4 + u
                 p = far_base + g
-                place = p - (wide - pixels)
-                meet(visit_ref[g], refs_ref[ref_at(visit_ints_s, p)], visit_sums_ref, place)
+                held = refs_ref[ref_at(visit_ints_s, p)]
+                meet(visit_spec_ref[g], held, visit_sums_ref, p - shift_lanes)
             return carry
 
-        lax.fori_loop(0, cap // 4, some, 0)
+        for refs_ref, least, most in ((far_ref, 0, cap), (far_pair_ref, cap, 2 * cap)):
+            a, b = max(low, least), min(high, most)
+            if b > a:
+                lax.fori_loop(a // 4, b // 4, functools.partial(some, refs_ref), 0)
 
     def transform(low, high):
         def some(step, carry):
@@ -580,53 +605,76 @@
             def put(n, rows, value):
                 spec_ref[base + n, rows] = value
 
-            spectra([base + n for n in range(4)], put)
+            four = [base + n for n in range(4)]
+            spectra([patch_ref[s] for s in four], [factor_ref[s] for s in four], put)
             return carry
 
         lax.fori_loop(0, (high - low) // 4, some, 0)
 
-    def transform_guests(low, high):
+    def transform_visit(low, high):
         def some(step, carry):
             base = low + step * 4
 
             def put(n, rows, value):
-                guest_ref[base + n, rows] = value.astype(BF16)
-
-            spectra([slot_at(far_base + base + n) for n in range(4)], put)
+                visit_spec_ref[base + n, rows] = value
+
+            four = [base + n for n in range(4)]
+            spectra(
+                [visit_ref[g] for g in four],
+                [visit_factor_ref[far_base - shift_lanes + g] for g in four],
+                put,
+            )
             return carry
 
         lax.fori_loop(0, (high - low) // 4, some, 0)
 
+    def pack(g, carry):
+        guest_ref[g] = patch_ref[slot_at(far_base + g)]
+        return carry
+
+    for load in load_tables[:fold_tables]:
+        load.wait()
     fold(0)
-    pl.semaphore_wait(barrier, devices - 1)
+    fold(1)
+
+    @pl.when(inner)
+    def _():
+        pl.semaphore_wait(barrier, 3)
+
+    @pl.when(outer)
+    def _():
+        pl.semaphore_wait(barrier, 2)
+
+    send_own(0)
+    for c in range(2, chunks):
+        fold(c)
+        send_own(c - 1)
     route()
-    send_own(0)
-    for c in range(1, chunks):
-        fold(c)
-        if c > 1:
-            send_own(c - 1)
     ints_load = pltpu.make_async_copy(ints_ref, ints_s, load_sem.at[chunks + 1])
     ints_load.start()
-
-    @pl.when(outer)
-    def _():
-        ints_copy.start()
-
     sums_ref[...] = jnp.zeros_like(sums_ref)
     visit_sums_ref[...] = jnp.zeros_like(visit_sums_ref)
+    send_own(chunks - 1)
     place_nodes()
-    if chunks > 1:
-        send_own(chunks - 1)
-    lax.fori_loop(0, slots // block_slots, factors, 0)
     load_patch.wait()
     ints_load.wait()
 
     @pl.when(outer)
     def _():
-        for g in range(GUEST_CHUNKS):
-            transform_guests(g * per_guest, (g + 1) * per_guest)
-            if g > 0:
-                guest_copy(g - 1).start()
+        lax.fori_loop(0, guests, pack, 0, unroll=4)
+
+    lax.fori_loop(
+        0, slots // block_slots, functools.partial(factors, cols_ref, factor_ref), 0
+    )
+
+    @pl.when(outer)
+    def _():
+        meta_copy.start()
+        for g in range(guest_chunks):
+            guest_copy(g).start()
+
+    for load in load_tables[fold_tables:]:
+        load.wait()
 
     def pass_on(c):
         flow(NEAR, c).wait_recv()
@@ -645,10 +693,6 @@
     done = 0
     for n in range(segments):
         transform(n * seg, (n + 1) * seg)
-        if n == 0:
-            @pl.when(outer)
-            def _():
-                guest_copy(GUEST_CHUNKS - 1).start()
         upto = chunks * (n + 1) // segments
         while done < upto:
             pass_on(done)
@@ -676,50 +720,77 @@
 
     visit_load = pltpu.make_async_copy(visit_ints_ref, visit_ints_s, load_sem.at[chunks + 2])
     ones = jnp.ones((8, pixels), F32)
+    row16 = lax.broadcasted_iota(jnp.int32, (16, slots), 0)
+    area = 1.0 / (pixels * pixels)
+    scale = jnp.where(row8 == 0, area, 2.0 * area * step_angle)
+
+    def gather_rows(from_ref):
+        parts = [exact(ones, from_ref[k], (((1,), (1,)), ((), ()))) for k in range(3)]
+        row = lax.broadcasted_iota(jnp.int32, parts[0].shape, 0)
+        return jnp.where(row == 0, parts[0], jnp.where(row == 1, parts[1], parts[2])) * scale[:, 0:1]
+
+    def gradient(on_tilt, terms, node_ref, first):
+        for axis in range(2):
+            coef = jnp.where(on_tilt, terms[1 + axis : 2 + axis], 0.0)
+            grad = exact(coef, node_ref[...])[:tilt_dev]
+            at = slice(axis * node_count, (axis + 1) * node_count)
+            grad_ref[:, at] = grad if first else grad_ref[:, at] + grad
+
+    def welcome():
+        meta_copy.wait_recv()
+        meta = visit_meta_ref[...]
+        visit_ints_ref[...] = (meta + 0.5).astype(jnp.int32)
+        visit_load.start()
+        block = jnp.concatenate(
+            [meta[:, shift_lanes:], jnp.zeros((pixels - 8, pixels), F32)], axis=0
+        )
+        visit_cols_ref[...] = block.T
+        visit_node_ref[...] = node_weights_of(visit_cols_ref)
+        first = (far_base - shift_lanes) // block_slots
+        last = first + guests // block_slots
+        lax.fori_loop(
+            first, last, functools.partial(factors, visit_cols_ref, visit_factor_ref), 0
+        )
+        visit_load.wait()
+
+    def bring_far(c):
+        flow(ON_FAR, c).wait_recv()
+        flow(FAR_PAIR, c).start()
 
     @pl.when(inner)
     def _():
-        ints_copy.wait_recv()
-        visit_load.start()
-        visit_load.wait()
-        for c in range(chunks):
-            flow(ON_FAR, c).wait_recv()
-            flow(FAR_PAIR, c).start()
+        welcome()
+        brought = 0
+        for g in range(guest_chunks - 1):
+            upto = chunks * (g + 1) // (guest_chunks - 1)
+            while brought < min(upto, chunks - 1):
+                bring_far(brought)
+                brought += 1
+            guest_copy(g).wait_recv()
+            transform_visit(guest_bounds[g], guest_bounds[g + 1])
+        bring_far(chunks - 1)
         process(far_ref, 6)
         for c in range(chunks):
             flow(FAR_PAIR, c).wait_recv()
         process(far_pair_ref, 7)
-        for g in range(GUEST_CHUNKS):
-            guest_copy(g).wait_recv()
-        entertain(far_ref, 0)
-        entertain(far_pair_ref, 1)
-        parts = [exact(ones, visit_sums_ref[k], (((1,), (1,)), ((), ()))) for k in range(3)]
-        back_ref[...] = jnp.where(row8 == 0, parts[0], jnp.where(row8 == 1, parts[1], parts[2]))
+        entertain(0, guest_bounds[guest_chunks - 1])
+
+    terms = exact(gather_rows(sums_ref), match_ref[...], (((1,), (1,)), ((), ())))
+    on_tilt = row16 == tilt_ref[...]
+    gradient(on_tilt, terms, node_ref, True)
+
+    @pl.when(inner)
+    def _():
+        guest_copy(guest_chunks - 1).wait_recv()
+        transform_visit(guest_bounds[guest_chunks - 1], guests)
+        entertain(guest_bounds[guest_chunks - 1], guests)
+        back = gather_rows(visit_sums_ref)
+        back_ref[...] = back
+        invited = visit_meta_ref[0:1, shift_lanes:] > 0.5
+        visit_tilt = jnp.where(invited, jnp.floor(visit_meta_ref[5:6, shift_lanes:] + 0.5), -1.0)
+        row = lax.broadcasted_iota(jnp.int32, (16, pixels), 0).astype(F32)
+        gradient(row == visit_tilt, back, visit_node_ref, False)
         back_copy.start()
-
-    parts = [exact(ones, sums_ref[k], (((1,), (1,)), ((), ()))) for k in range(3)]
-    row_wide = lax.broadcasted_iota(jnp.int32, (8, wide), 0)
-    mixed = jnp.where(row_wide == 0, parts[0], jnp.where(row_wide == 1, parts[1], parts[2]))
-    cols_ref[:8, :] = jnp.zeros((8, slots), F32)
-
-    @pl.when(outer)
-    def _():
-        back_copy.wait_recv()
-        cols_ref[:8, :] = back_in_ref[...]
-
-    mixed = jnp.concatenate(
-        [mixed[:, : wide - pixels], mixed[:, wide - pixels :] + cols_ref[:8, :]], axis=1
-    )
-    area = 1.0 / (pixels * pixels)
-    mixed = mixed * jnp.where(row_wide == 0, area, 2.0 * area * step_angle)
-    terms = exact(mixed, match_ref[...], (((1,), (1,)), ((), ())))
-    terms_ref[...] = terms[:3]
-    row16 = lax.broadcasted_iota(jnp.int32, (16, slots), 0)
-    on_tilt = row16 == tilt_ref[...]
-    for axis in range(2):
-        coef = jnp.where(on_tilt, terms[1 + axis : 2 + axis], 0.0)
-        grad = exact(coef, node_ref[...])
-        grad_ref[:, axis * node_count : (axis + 1) * node_count] = grad[:tilt_dev]
 
     def grad_copy(hop):
         return remote(
@@ -727,8 +798,6 @@
             lax.rem(me + hop, devices),
         )
 
-    for hop in range(1, devices):
-        grad_copy(hop).start()
     for c in range(chunks):
         flow(OWN, c).wait_send()
         flow(NEAR, c).wait_send()
@@ -742,13 +811,30 @@
             flow(ON_FAR, c).wait_send()
             flow(ON_OPP, c).wait_send()
             flow(FAR_PAIR, c).wait_send()
+
+    @pl.when(outer)
+    def _():
+        meta_copy.wait_send()
+        for g in range(guest_chunks):
+            guest_copy(g).wait_send()
+
+    for hop in range(1, devices):
+        grad_copy(hop).start()
+    back_in = jnp.zeros((8, pixels), F32)
+    cols_ref[:8, :] = back_in
+
+    @pl.when(outer)
+    def _():
+        back_copy.wait_recv()
+        cols_ref[:8, :] = back_in_ref[...]
+
+    terms = terms + exact(cols_ref[:8, :], match_ref[:, shift_lanes:], (((1,), (1,)), ((), ())))
+    for index in range(3):
+        terms_ref[index] = terms[index : index + 1]
+
+    @pl.when(inner)
+    def _():
         back_copy.wait_send()
-
-    @pl.when(outer)
-    def _():
-        ints_copy.wait_send()
-        for g in range(GUEST_CHUNKS):
-            guest_copy(g).wait_send()
 
     for hop in range(1, devices):
         grad_copy(hop).wait()
@@ -772,8 +858,12 @@
     devices = CHIPS * CORES
     cap = 3 * slots // (2 * devices)
     refs = view_dev * tilt_dev
-    chunks = math.gcd(refs, 5)
+    per = refs // math.gcd(refs, 5)
+    bounds = sorted({0, per // 4, per // 2} | set(range(per, refs + 1, per)))
+    chunks = len(bounds) - 1
     guests = CORES * cap
+    guest_bounds = [0, guests // 3, 2 * guests // 3, 11 * guests // 12, guests]
+    guest_chunks = len(guest_bounds) - 1
     wide = 2 * pixels
     rows = pixels + EXTRA_ROWS
     spec_rows = pixels + 2 * EXTRA_ROWS
@@ -781,16 +871,21 @@
     anywhere = pl.BlockSpec(memory_space=pl.ANY)
     dma = pltpu.SemaphoreType.DMA
     block = pltpu.VMEM((refs, rows, pixels), BF16)
-    scratch = [
+    held_tables = tables(pixels)
+    scratch = [pltpu.VMEM(x.shape, x.dtype) for x in held_tables] + [
         pltpu.VMEM((slots, pixels, pixels), BF16),
         pltpu.VMEM((refs, 2, pixels, pixels), BF16),
     ] + [block] * 8 + [
-        pltpu.VMEM((guests, spec_rows, pixels), BF16),
-        pltpu.VMEM((guests, spec_rows, pixels), BF16),
+        pltpu.VMEM((guests, pixels, pixels), BF16),
+        pltpu.VMEM((guests, pixels, pixels), BF16),
         pltpu.VMEM((slots, spec_rows, pixels), F32),
+        pltpu.VMEM((guests, spec_rows, pixels), F32),
         pltpu.VMEM((slots, 16, pixels), F32),
+        pltpu.VMEM((pixels, 16, pixels), F32),
         pltpu.VMEM((slots, slots), F32),
+        pltpu.VMEM((pixels, pixels), F32),
         pltpu.VMEM((slots, node_count), F32),
+        pltpu.VMEM((pixels, node_count), F32),
         pltpu.VMEM((slots, wide), F32),
         pltpu.VMEM((3, wide, pixels), F32),
         pltpu.VMEM((3, pixels, pixels), F32),
@@ -798,27 +893,30 @@
         pltpu.VMEM((8, wide), jnp.int32),
         pltpu.SMEM((8, wide), jnp.int32),
         pltpu.SMEM((8, wide), jnp.int32),
+        pltpu.VMEM((8, wide), F32),
+        pltpu.VMEM((8, wide), F32),
         pltpu.VMEM((tilt_dev, 2 * node_count), F32),
         pltpu.VMEM((devices - 1, tilt_dev, 2 * node_count), F32),
         pltpu.VMEM((8, pixels), F32),
         pltpu.VMEM((8, pixels), F32),
         dma((chunks + 3,)),
+        dma((len(held_tables),)),
         dma((8, chunks)),
         dma((8, chunks)),
-        dma((GUEST_CHUNKS,)),
-        dma((GUEST_CHUNKS,)),
+        dma((guest_chunks,)),
+        dma((guest_chunks,)),
         dma((2,)),
         dma((2,)),
         dma((devices - 1,)),
         dma((devices - 1,)),
     ]
     terms, new_warp = pl.pallas_call(
-        functools.partial(gather_kernel, cap, view_dev, chunks),
+        functools.partial(gather_kernel, cap, view_dev, bounds, guest_bounds),
         out_shape=(
-            jax.ShapeDtypeStruct((3, slots), F32),
-            jax.ShapeDtypeStruct(warp_grid.shape, F32),
+            pltpu.VMEM((3, 1, slots), F32),
+            pltpu.VMEM(warp_grid.shape, F32),
         ),
-        in_specs=[vmem] * 5 + [anywhere] * 2 + [vmem] * 8,
+        in_specs=[vmem] * 5 + [anywhere] * 10,
         out_specs=(vmem, vmem),
         scratch_shapes=scratch,
         compiler_params=pltpu.CompilerParams(
@@ -827,9 +925,9 @@
         name="gather_sums",
     )(
         slot_view.reshape(1, slots), slot_tilt, slot_pos.reshape(2, slots), defocus, warp_grid,
-        patches[0], projections.reshape(refs, 2, pixels, pixels), *tables(pixels),
-    )
-    return (terms[:, None, :], new_warp)
+        patches[0], projections.reshape(refs, 2, pixels, pixels), *held_tables,
+    )
+    return (terms, new_warp)
 
 
 def solution(mesh):

time: 91.2 us -> 83 us (0.910)
  Pallas kernels: 87.8 us -> 81 us
  local copies, waits for them, and re-layouts: 2.57 us -> 1.17 us
    pallas_call x1, Pallas kernels: 87.8 us -> 81 us  [on_device_gathered(): pl.pallas_call(functools.partial(gather_kernel, cap, view_dev, bounds, gu...]
    unnamed x2, local copies, waits for them, and re-layouts: 2.57 us -> 1.17 us
where the time goes in v2:
time: 83 us; the launch traced here: 82.8 us
  Pallas kernels  81 us (98%)
  local copies, waits for them, and re-layouts  1.17 us (1%)
    pallas_call x1, Pallas kernels, on_device_gathered(): pl.pallas_call(functools.partial(gather_kernel, cap, view_dev, bounds, gu...  81 us

profile of v2, /device:TPU:0, one launch (start us, length us, event | category | flops | bytes accessed | tf_op | source)
XLA Modules:
  0.0 82.8 jit_solution(11320526556905139173)
XLA Ops:
  0.6 81.0 %gather_sums.1 = (f32[3,1,128]{2,1,0:T(1,128)S(1)}, f32[10,2,256]{2,1,0:T(2,128)S(1)}) custom-call(s32[1,128]{1,0:T(1,128)} %bitcast.6, s32[1,128]{1,0:T(1,128)} %tilt_ref.1, bf16[2,128]{1,0:T(2,128)(2,1)} %bitcast.7, bf16[1,128]{1,0:T(2,128)(2,1)} %focus_ref.1, f32[10,2,256]{2,1,0:T(2,128)} %warp_ref.1, bf16[128,128,128]{2,1,0:T(8,128)(2,1)} %bitcast.4, ...), custom_call_target="tpu_custom_call" | custom-call | tf_op jit(solution)/shard_map/gather_sums/pallas_call | solution.py:913
  81.6 0.6 copy.19
  82.2 0.6 copy.20

commit v3 on v2

--- a/solution.py
+++ b/solution.py
@@ -268,11 +268,12 @@
                   flip_hbm, unit_hbm, waves_hbm, levels_hbm, terms_ref, new_ref, first_ref,
                   second_ref, edge_ref, turn_ref, flip_ref, unit_ref, waves_ref, levels_ref,
                   patch_ref, proj_ref, own_ref, pair_ref, near_ref, near_pair_ref, opp_ref,
-                  opp_pair_ref, far_ref, far_pair_ref, guest_ref, visit_ref, spec_ref,
+                  opp_pair_ref, far_ref, far_pair_ref, guest_ref, visit_ref, guest_last_ref,
+                  visit_last_ref, spec_ref,
                   visit_spec_ref, factor_ref, visit_factor_ref, cols_ref, visit_cols_ref,
                   node_ref, visit_node_ref, match_ref, sums_ref, visit_sums_ref, ints_ref,
                   visit_ints_ref, ints_s, visit_ints_s, meta_ref, visit_meta_ref, grad_ref,
-                  held_ref, back_ref, back_in_ref, load_sem, table_sem, send_sem, recv_sem,
+                  sent_ref, held_ref, back_ref, back_in_ref, load_sem, table_sem, send_sem, recv_sem,
                   guest_send, guest_recv, misc_send, misc_recv, grad_send, grad_recv):
     slots, pixels = patch_ref.shape[0], patch_ref.shape[1]
     half = pixels // 2
@@ -282,6 +283,7 @@
     chunks = len(bounds) - 1
     guests = guest_ref.shape[0]
     guest_chunks = len(guest_bounds) - 1
+    last_guest = guest_bounds[guest_chunks - 1]
     devices = CHIPS * CORES
     padded = devices * cap
     far_base = padded - guests
@@ -353,6 +355,10 @@
         )
 
     def guest_copy(g):
+        if g == guest_chunks - 1:
+            return remote(
+                guest_last_ref, visit_last_ref, guest_send.at[g], guest_recv.at[g], mate
+            )
         rows = pl.ds(guest_bounds[g], guest_bounds[g + 1] - guest_bounds[g])
         return remote(
             guest_ref.at[rows], visit_ref.at[rows], guest_send.at[g], guest_recv.at[g], mate
@@ -435,14 +441,18 @@
 
     def place_nodes():
         weights = node_weights_of(cols_ref)
-        node_ref[...] = weights
         hits = jnp.where(cols_ref[:, 5:6] == lane_f[:, :16], 1.0, 0.0)
         spare = jnp.zeros((16 - tilt_dev, node_count), F32)
         for axis in range(2):
             grid = jnp.concatenate([warp_ref[:, axis, :], spare], axis=0)
             shift = jnp.sum(exact(hits, grid) * weights, axis=1, keepdims=True)
             cols_ref[:, 6 + axis : 7 + axis] = shift
-        meta_ref[...] = exact(cols_ref[...].T[:8], match_ref[...])
+        meta = exact(cols_ref[...].T[:8], match_ref[...])
+        meta_ref[...] = meta
+        spare = jnp.zeros((pixels - 8, pixels), F32)
+        for at in range(0, wide, pixels):
+            cols = jnp.concatenate([meta[:, at : at + pixels], spare], axis=0).T
+            node_ref[at : at + pixels] = node_weights_of(cols)
 
     step_angle = 2.0 * math.pi / pixels
     norm = 1.0 / (half * half)
@@ -554,7 +564,7 @@
     def stack(x):
         return jnp.sum(x.reshape(half // 8, 8, pixels), axis=0)
 
-    def meet(y, ref, out_ref, place):
+    def compare(y, ref):
         y = y.astype(F32)
         r = ref.astype(F32)
         y_re, y_im, straight = y[:half], y[half:pixels], y[pixels : pixels + 8]
@@ -566,8 +576,13 @@
         energy = jnp.where((row8 == 4) | (row8 == 5), crossed, 0.0) - 2.0 * match
         grad_x = stack(swirl) * line + edge * weight_x
         grad_y = stack(swirl * freq_y) + edge * weight_y
-        for index, value in enumerate((energy, grad_x, grad_y)):
+        return energy, grad_x, grad_y
+
+    def meet(y, ref, out_ref, place):
+        found = compare(y, ref)
+        for index, value in enumerate(found):
             out_ref[index, pl.ds(place, 1)] = jnp.sum(value, axis=0, keepdims=True)
+        return found
 
     def slot_at(p):
         return jnp.clip(ints_s[0, p], 0, slots - 1)
@@ -661,7 +676,7 @@
 
     @pl.when(outer)
     def _():
-        lax.fori_loop(0, guests, pack, 0, unroll=4)
+        lax.fori_loop(0, last_guest, pack, 0, unroll=4)
 
     lax.fori_loop(
         0, slots // block_slots, functools.partial(factors, cols_ref, factor_ref), 0
@@ -670,7 +685,7 @@
     @pl.when(outer)
     def _():
         meta_copy.start()
-        for g in range(guest_chunks):
+        for g in range(guest_chunks - 1):
             guest_copy(g).start()
 
     for load in load_tables[fold_tables:]:
@@ -698,7 +713,17 @@
             pass_on(done)
             done += 1
 
+    @pl.when(outer)
+    def _():
+        for g in range(last_guest, guests):
+            guest_last_ref[g - last_guest] = spec_ref[slot_at(far_base + g)].astype(BF16)
+
     process(own_ref, 0)
+
+    @pl.when(outer)
+    def _():
+        guest_copy(guest_chunks - 1).start()
+
     for c in range(chunks):
         flow(OWN, c).wait_recv()
     process(pair_ref, 1)
@@ -720,7 +745,6 @@
 
     visit_load = pltpu.make_async_copy(visit_ints_ref, visit_ints_s, load_sem.at[chunks + 2])
     ones = jnp.ones((8, pixels), F32)
-    row16 = lax.broadcasted_iota(jnp.int32, (16, slots), 0)
     area = 1.0 / (pixels * pixels)
     scale = jnp.where(row8 == 0, area, 2.0 * area * step_angle)
 
@@ -761,41 +785,50 @@
     def _():
         welcome()
         brought = 0
-        for g in range(guest_chunks - 1):
-            upto = chunks * (g + 1) // (guest_chunks - 1)
-            while brought < min(upto, chunks - 1):
+        for g in range(guest_chunks - 2):
+            while brought < chunks - guest_chunks + 2 + g:
                 bring_far(brought)
                 brought += 1
             guest_copy(g).wait_recv()
             transform_visit(guest_bounds[g], guest_bounds[g + 1])
-        bring_far(chunks - 1)
+        while brought < chunks:
+            bring_far(brought)
+            brought += 1
         process(far_ref, 6)
+        entertain(0, cap)
         for c in range(chunks):
             flow(FAR_PAIR, c).wait_recv()
         process(far_pair_ref, 7)
-        entertain(0, guest_bounds[guest_chunks - 1])
-
-    terms = exact(gather_rows(sums_ref), match_ref[...], (((1,), (1,)), ((), ())))
-    on_tilt = row16 == tilt_ref[...]
-    gradient(on_tilt, terms, node_ref, True)
-
-    @pl.when(inner)
-    def _():
-        guest_copy(guest_chunks - 1).wait_recv()
-        transform_visit(guest_bounds[guest_chunks - 1], guests)
-        entertain(guest_bounds[guest_chunks - 1], guests)
-        back = gather_rows(visit_sums_ref)
-        back_ref[...] = back
-        invited = visit_meta_ref[0:1, shift_lanes:] > 0.5
-        visit_tilt = jnp.where(invited, jnp.floor(visit_meta_ref[5:6, shift_lanes:] + 0.5), -1.0)
-        row = lax.broadcasted_iota(jnp.int32, (16, pixels), 0).astype(F32)
-        gradient(row == visit_tilt, back, visit_node_ref, False)
-        back_copy.start()
+        entertain(cap, guest_bounds[guest_chunks - 2])
+        guest_copy(guest_chunks - 2).wait_recv()
+        transform_visit(guest_bounds[guest_chunks - 2], last_guest)
+        entertain(guest_bounds[guest_chunks - 2], last_guest)
+
+    def tilts_at(meta):
+        tilt = jnp.where(meta[4:5] > 0.5, jnp.floor(meta[5:6] + 0.5), -1.0)
+        return lax.broadcasted_iota(jnp.int32, (16, meta.shape[1]), 0).astype(F32) == tilt
+
+    places = gather_rows(sums_ref)
+    gradient(tilts_at(meta_ref[...]), places, node_ref, True)
+
+    lane_blocks = range(0, 2 * node_count, pixels)
+
+    def pack_sent(value):
+        sent_ref[...] = jnp.concatenate(
+            [value[:, at : at + pixels] for at in lane_blocks], axis=0
+        ).astype(BF16)
 
     def grad_copy(hop):
         return remote(
-            grad_ref, held_ref.at[hop - 1], grad_send.at[hop - 1], grad_recv.at[hop - 1],
+            sent_ref, held_ref.at[hop - 1], grad_send.at[hop - 1], grad_recv.at[hop - 1],
             lax.rem(me + hop, devices),
+        )
+
+    @pl.when(inner)
+    def _():
+        gradient(
+            tilts_at(visit_meta_ref[:, shift_lanes:]), gather_rows(visit_sums_ref),
+            visit_node_ref, False,
         )
 
     for c in range(chunks):
@@ -817,9 +850,38 @@
         meta_copy.wait_send()
         for g in range(guest_chunks):
             guest_copy(g).wait_send()
+        pack_sent(grad_ref[...])
+
+    @pl.when(inner)
+    def _():
+        guest_copy(guest_chunks - 1).wait_recv()
+        total = [grad_ref[:, a * node_count : (a + 1) * node_count] for a in range(2)]
+        tilt_col = lax.broadcasted_iota(jnp.int32, (tilt_dev, 1), 0).astype(F32)
+        for g in range(last_guest, guests):
+            p = far_base + g
+            q = p - shift_lanes
+            held = far_pair_ref[ref_at(visit_ints_s, p)]
+            found = meet(visit_last_ref[g - last_guest], held, visit_sums_ref, q)
+            cols = visit_cols_ref[q : q + 1, :]
+            here = (jnp.abs(cols[:, 5:6] - tilt_col) < 0.5) & (cols[:, 4:5] > 0.5)
+            weights = visit_node_ref[q : q + 1, :]
+            for axis in range(2):
+                value = jnp.sum(found[1 + axis], axis=(0, 1), keepdims=True)
+                value = value * (2.0 * area * step_angle)
+                total[axis] = total[axis] + jnp.where(here, value, 0.0) * weights
+        for axis in range(2):
+            at = slice(axis * node_count, (axis + 1) * node_count)
+            grad_ref[:, at] = total[axis]
+        pack_sent(jnp.concatenate(total, axis=1))
 
     for hop in range(1, devices):
         grad_copy(hop).start()
+
+    @pl.when(inner)
+    def _():
+        back_ref[...] = gather_rows(visit_sums_ref)
+        back_copy.start()
+
     back_in = jnp.zeros((8, pixels), F32)
     cols_ref[:8, :] = back_in
 
@@ -828,7 +890,10 @@
         back_copy.wait_recv()
         cols_ref[:8, :] = back_in_ref[...]
 
-    terms = terms + exact(cols_ref[:8, :], match_ref[:, shift_lanes:], (((1,), (1,)), ((), ())))
+    places = jnp.concatenate(
+        [places[:, :shift_lanes], places[:, shift_lanes:] + cols_ref[:8, :]], axis=1
+    )
+    terms = exact(places, match_ref[...], (((1,), (1,)), ((), ())))
     for index in range(3):
         terms_ref[index] = terms[index : index + 1]
 
@@ -838,9 +903,12 @@
 
     for hop in range(1, devices):
         grad_copy(hop).wait()
-    total = grad_ref[...]
-    for hop in range(1, devices):
-        total = total + held_ref[hop - 1]
+    others = held_ref[0].astype(F32)
+    for hop in range(2, devices):
+        others = others + held_ref[hop - 1].astype(F32)
+    total = grad_ref[...] + jnp.concatenate(
+        [others[n * tilt_dev : (n + 1) * tilt_dev] for n in range(len(lane_blocks))], axis=1
+    )
     change = total / jnp.sqrt(total * total + TRUST_FLOOR * TRUST_FLOOR)
     for axis in range(2):
         at = slice(axis * node_count, (axis + 1) * node_count)
@@ -857,12 +925,15 @@
     node_count = warp_grid.shape[2]
     devices = CHIPS * CORES
     cap = 3 * slots // (2 * devices)
+    if slots != pixels or cap % 24 or node_count != GRID * GRID:
+        return on_device(
+            patches, slot_view, slot_tilt, slot_pos, defocus, projections, warp_grid
+        )
     refs = view_dev * tilt_dev
-    per = refs // math.gcd(refs, 5)
-    bounds = sorted({0, per // 4, per // 2} | set(range(per, refs + 1, per)))
+    bounds = sorted({refs * n // 40 for n in (0, 1, 2, 4, 7, 12, 20, 28, 36, 40)})
     chunks = len(bounds) - 1
     guests = CORES * cap
-    guest_bounds = [0, guests // 3, 2 * guests // 3, 11 * guests // 12, guests]
+    guest_bounds = [guests * n // 12 for n in (0, 4, 7, 9, 10, 11, 12)]
     guest_chunks = len(guest_bounds) - 1
     wide = 2 * pixels
     rows = pixels + EXTRA_ROWS
@@ -878,13 +949,15 @@
     ] + [block] * 8 + [
         pltpu.VMEM((guests, pixels, pixels), BF16),
         pltpu.VMEM((guests, pixels, pixels), BF16),
+        pltpu.VMEM((guests - guest_bounds[-2], spec_rows, pixels), BF16),
+        pltpu.VMEM((guests - guest_bounds[-2], spec_rows, pixels), BF16),
         pltpu.VMEM((slots, spec_rows, pixels), F32),
         pltpu.VMEM((guests, spec_rows, pixels), F32),
         pltpu.VMEM((slots, 16, pixels), F32),
         pltpu.VMEM((pixels, 16, pixels), F32),
         pltpu.VMEM((slots, slots), F32),
         pltpu.VMEM((pixels, pixels), F32),
-        pltpu.VMEM((slots, node_count), F32),
+        pltpu.VMEM((wide, node_count), F32),
         pltpu.VMEM((pixels, node_count), F32),
         pltpu.VMEM((slots, wide), F32),
         pltpu.VMEM((3, wide, pixels), F32),
@@ -896,7 +969,8 @@
         pltpu.VMEM((8, wide), F32),
         pltpu.VMEM((8, wide), F32),
         pltpu.VMEM((tilt_dev, 2 * node_count), F32),
-        pltpu.VMEM((devices - 1, tilt_dev, 2 * node_count), F32),
+        pltpu.VMEM((2 * node_count // pixels * tilt_dev, pixels), BF16),
+        pltpu.VMEM((devices - 1, 2 * node_count // pixels * tilt_dev, pixels), BF16),
         pltpu.VMEM((8, pixels), F32),
         pltpu.VMEM((8, pixels), F32),
         dma((chunks + 3,)),

time: 83 us -> 79.3 us (0.955)
  Pallas kernels: 81 us -> 77.3 us
    pallas_call x1, Pallas kernels: 81 us -> 77.3 us  [on_device_gathered(): pl.pallas_call(functools.partial(gather_kernel, cap, view_dev, bounds, gu...]
where the time goes in v3:
time: 79.3 us; the launch traced here: 79.1 us
  Pallas kernels  77.3 us (97%)
  local copies, waits for them, and re-layouts  1.17 us (1%)
    pallas_call x1, Pallas kernels, on_device_gathered(): pl.pallas_call(functools.partial(gather_kernel, cap, view_dev, bounds, gu...  77.3 us

profile of v3, /device:TPU:0, one launch (start us, length us, event | category | flops | bytes accessed | tf_op | source)
XLA Modules:
  0.0 79.1 jit_solution(13743557210365921317)
XLA Ops:
  0.6 77.3 %gather_sums.1 = (f32[3,1,128]{2,1,0:T(1,128)S(1)}, f32[10,2,256]{2,1,0:T(2,128)S(1)}) custom-call(s32[1,128]{1,0:T(1,128)} %bitcast.6, s32[1,128]{1,0:T(1,128)} %tilt_ref.1, bf16[2,128]{1,0:T(2,128)(2,1)} %bitcast.7, bf16[1,128]{1,0:T(2,128)(2,1)} %focus_ref.1, f32[10,2,256]{2,1,0:T(2,128)} %warp_ref.1, bf16[128,128,128]{2,1,0:T(8,128)(2,1)} %bitcast.4, ...), custom_call_target="tpu_custom_call" | custom-call | tf_op jit(solution)/shard_map/gather_sums/pallas_call | solution.py:987
  77.9 0.6 copy.19
  78.5 0.6 copy.20

commit v4 on v3

--- a/solution.py
+++ b/solution.py
@@ -273,7 +273,7 @@
                   visit_spec_ref, factor_ref, visit_factor_ref, cols_ref, visit_cols_ref,
                   node_ref, visit_node_ref, match_ref, sums_ref, visit_sums_ref, ints_ref,
                   visit_ints_ref, ints_s, visit_ints_s, meta_ref, visit_meta_ref, grad_ref,
-                  sent_ref, held_ref, back_ref, back_in_ref, load_sem, table_sem, send_sem, recv_sem,
+                  sent_ref, mate_grad_ref, held_ref, back_ref, back_in_ref, load_sem, table_sem, send_sem, recv_sem,
                   guest_send, guest_recv, misc_send, misc_recv, grad_send, grad_recv):
     slots, pixels = patch_ref.shape[0], patch_ref.shape[1]
     half = pixels // 2
@@ -813,23 +813,39 @@
 
     lane_blocks = range(0, 2 * node_count, pixels)
 
-    def pack_sent(value):
-        sent_ref[...] = jnp.concatenate(
-            [value[:, at : at + pixels] for at in lane_blocks], axis=0
-        ).astype(BF16)
-
-    def grad_copy(hop):
+    def pack_sent(value, more=0.0):
+        packed = jnp.concatenate([value[:, at : at + pixels] for at in lane_blocks], axis=0)
+        sent_ref[...] = (packed + more).astype(BF16)
+
+    mate_grad = remote(sent_ref, mate_grad_ref, misc_send.at[2], misc_recv.at[2], mate)
+
+    places_to = [
+        place * CORES + other
+        for place in (CHIPS - 1 - mate_chip, CHIPS - 1 - chip, mate_chip)
+        for other in (core, 1 - core)
+    ] + [partner]
+
+    def grad_copy(n):
+        slot = me - CORES
         return remote(
-            sent_ref, held_ref.at[hop - 1], grad_send.at[hop - 1], grad_recv.at[hop - 1],
-            lax.rem(me + hop, devices),
-        )
+            sent_ref, held_ref.at[slot], grad_send.at[n], grad_recv.at[slot], places_to[n]
+        )
+
+    def grad_from(sender):
+        slot = sender - CORES
+        return remote(
+            sent_ref, held_ref.at[slot], grad_send.at[slot], grad_recv.at[slot], partner
+        )
+
+    @pl.when(outer)
+    def _():
+        pack_sent(grad_ref[...])
 
     @pl.when(inner)
     def _():
-        gradient(
-            tilts_at(visit_meta_ref[:, shift_lanes:]), gather_rows(visit_sums_ref),
-            visit_node_ref, False,
-        )
+        early = gather_rows(visit_sums_ref)
+        back_ref[...] = early
+        gradient(tilts_at(visit_meta_ref[:, shift_lanes:]), early, visit_node_ref, False)
 
     for c in range(chunks):
         flow(OWN, c).wait_send()
@@ -847,72 +863,84 @@
 
     @pl.when(outer)
     def _():
+        mate_grad.start()
         meta_copy.wait_send()
         for g in range(guest_chunks):
             guest_copy(g).wait_send()
-        pack_sent(grad_ref[...])
 
     @pl.when(inner)
     def _():
         guest_copy(guest_chunks - 1).wait_recv()
         total = [grad_ref[:, a * node_count : (a + 1) * node_count] for a in range(2)]
         tilt_col = lax.broadcasted_iota(jnp.int32, (tilt_dev, 1), 0).astype(F32)
+        back = back_ref[...]
         for g in range(last_guest, guests):
             p = far_base + g
             q = p - shift_lanes
             held = far_pair_ref[ref_at(visit_ints_s, p)]
-            found = meet(visit_last_ref[g - last_guest], held, visit_sums_ref, q)
+            found = compare(visit_last_ref[g - last_guest], held)
             cols = visit_cols_ref[q : q + 1, :]
             here = (jnp.abs(cols[:, 5:6] - tilt_col) < 0.5) & (cols[:, 4:5] > 0.5)
             weights = visit_node_ref[q : q + 1, :]
+            values = [jnp.sum(x, axis=(0, 1), keepdims=True) for x in found]
+            values = [values[0] * area] + [v * (2.0 * area * step_angle) for v in values[1:]]
             for axis in range(2):
-                value = jnp.sum(found[1 + axis], axis=(0, 1), keepdims=True)
-                value = value * (2.0 * area * step_angle)
-                total[axis] = total[axis] + jnp.where(here, value, 0.0) * weights
-        for axis in range(2):
-            at = slice(axis * node_count, (axis + 1) * node_count)
-            grad_ref[:, at] = total[axis]
-        pack_sent(jnp.concatenate(total, axis=1))
-
-    for hop in range(1, devices):
-        grad_copy(hop).start()
+                total[axis] = total[axis] + jnp.where(here, values[1 + axis], 0.0) * weights
+            for index in range(3):
+                back = jnp.where((row8 == index) & (lane == q), values[index], back)
+        mate_grad.wait_recv()
+        pack_sent(jnp.concatenate(total, axis=1), mate_grad_ref[...].astype(F32))
+        back_ref[...] = back
+        held_ref[me - CORES] = sent_ref[...]
 
     @pl.when(inner)
     def _():
-        back_ref[...] = gather_rows(visit_sums_ref)
+        for n in range(devices - 1):
+            grad_copy(n).start()
         back_copy.start()
 
-    back_in = jnp.zeros((8, pixels), F32)
-    cols_ref[:8, :] = back_in
-
-    @pl.when(outer)
-    def _():
-        back_copy.wait_recv()
-        cols_ref[:8, :] = back_in_ref[...]
-
-    places = jnp.concatenate(
-        [places[:, :shift_lanes], places[:, shift_lanes:] + cols_ref[:8, :]], axis=1
-    )
-    terms = exact(places, match_ref[...], (((1,), (1,)), ((), ())))
-    for index in range(3):
-        terms_ref[index] = terms[index : index + 1]
+    def put_terms(places):
+        terms = exact(places, match_ref[...], (((1,), (1,)), ((), ())))
+        for index in range(3):
+            terms_ref[index] = terms[index : index + 1]
 
     @pl.when(inner)
     def _():
-        back_copy.wait_send()
-
-    for hop in range(1, devices):
-        grad_copy(hop).wait()
-    others = held_ref[0].astype(F32)
-    for hop in range(2, devices):
-        others = others + held_ref[hop - 1].astype(F32)
-    total = grad_ref[...] + jnp.concatenate(
-        [others[n * tilt_dev : (n + 1) * tilt_dev] for n in range(len(lane_blocks))], axis=1
+        put_terms(places)
+
+    senders = range(CORES, devices - CORES)
+    for sender in senders:
+        @pl.when(me != sender)
+        def _():
+            grad_from(sender).wait_recv()
+
+    packed = held_ref[0].astype(F32)
+    for n in range(1, len(senders)):
+        packed = packed + held_ref[n].astype(F32)
+    total = jnp.concatenate(
+        [packed[n * tilt_dev : (n + 1) * tilt_dev] for n in range(len(lane_blocks))], axis=1
     )
     change = total / jnp.sqrt(total * total + TRUST_FLOOR * TRUST_FLOOR)
     for axis in range(2):
         at = slice(axis * node_count, (axis + 1) * node_count)
         new_ref[:, axis, :] = warp_ref[:, axis, :] - change[:, at]
+
+    @pl.when(outer)
+    def _():
+        back_copy.wait_recv()
+        put_terms(
+            jnp.concatenate(
+                [places[:, :shift_lanes], places[:, shift_lanes:] + back_in_ref[...]], axis=1
+            )
+        )
+
+        mate_grad.wait_send()
+
+    @pl.when(inner)
+    def _():
+        back_copy.wait_send()
+        for n in range(devices - 1):
+            grad_copy(n).wait_send()
 
 
 def on_device_gathered(
@@ -970,7 +998,8 @@
         pltpu.VMEM((8, wide), F32),
         pltpu.VMEM((tilt_dev, 2 * node_count), F32),
         pltpu.VMEM((2 * node_count // pixels * tilt_dev, pixels), BF16),
-        pltpu.VMEM((devices - 1, 2 * node_count // pixels * tilt_dev, pixels), BF16),
+        pltpu.VMEM((2 * node_count // pixels * tilt_dev, pixels), BF16),
+        pltpu.VMEM((devices - 2 * CORES, 2 * node_count // pixels * tilt_dev, pixels), BF16),
         pltpu.VMEM((8, pixels), F32),
         pltpu.VMEM((8, pixels), F32),
         dma((chunks + 3,)),
@@ -979,10 +1008,10 @@
         dma((8, chunks)),
         dma((guest_chunks,)),
         dma((guest_chunks,)),
-        dma((2,)),
-        dma((2,)),
+        dma((3,)),
+        dma((3,)),
         dma((devices - 1,)),
-        dma((devices - 1,)),
+        dma((devices - 2 * CORES,)),
     ]
     terms, new_warp = pl.pallas_call(
         functools.partial(gather_kernel, cap, view_dev, bounds, guest_bounds),

time: 79.3 us -> 79.6 us (level)
  no operation moved by 1% of the time
where the time goes in v4:
time: 79.6 us; the launch traced here: 79.4 us
  Pallas kernels  77.6 us (97%)
  local copies, waits for them, and re-layouts  1.17 us (1%)
    pallas_call x1, Pallas kernels, on_device_gathered(): pl.pallas_call(functools.partial(gather_kernel, cap, view_dev, bounds, gu...  77.6 us

profile of v4, /device:TPU:0, one launch (start us, length us, event | category | flops | bytes accessed | tf_op | source)
XLA Modules:
  0.0 79.4 jit_solution(9180143769955695969)
XLA Ops:
  0.6 77.6 %gather_sums.1 = (f32[3,1,128]{2,1,0:T(1,128)S(1)}, f32[10,2,256]{2,1,0:T(2,128)S(1)}) custom-call(s32[1,128]{1,0:T(1,128)} %bitcast.6, s32[1,128]{1,0:T(1,128)} %tilt_ref.1, bf16[2,128]{1,0:T(2,128)(2,1)} %bitcast.7, bf16[1,128]{1,0:T(2,128)(2,1)} %focus_ref.1, f32[10,2,256]{2,1,0:T(2,128)} %warp_ref.1, bf16[128,128,128]{2,1,0:T(8,128)(2,1)} %bitcast.4, ...), custom_call_target="tpu_custom_call" | custom-call | tf_op jit(solution)/shard_map/gather_sums/pallas_call | solution.py:1016
  78.2 0.6 copy.19
  78.8 0.6 copy.20

commit v5 on v4

--- a/solution.py
+++ b/solution.py
@@ -273,7 +273,7 @@
                   visit_spec_ref, factor_ref, visit_factor_ref, cols_ref, visit_cols_ref,
                   node_ref, visit_node_ref, match_ref, sums_ref, visit_sums_ref, ints_ref,
                   visit_ints_ref, ints_s, visit_ints_s, meta_ref, visit_meta_ref, grad_ref,
-                  sent_ref, mate_grad_ref, held_ref, back_ref, back_in_ref, load_sem, table_sem, send_sem, recv_sem,
+                  sent_ref, mate_grad_ref, pair_grad_ref, both_ref, held_ref, back_ref, back_in_ref, load_sem, table_sem, send_sem, recv_sem,
                   guest_send, guest_recv, misc_send, misc_recv, grad_send, grad_recv):
     slots, pixels = patch_ref.shape[0], patch_ref.shape[1]
     half = pixels // 2
@@ -819,23 +819,18 @@
 
     mate_grad = remote(sent_ref, mate_grad_ref, misc_send.at[2], misc_recv.at[2], mate)
 
-    places_to = [
-        place * CORES + other
-        for place in (CHIPS - 1 - mate_chip, CHIPS - 1 - chip, mate_chip)
-        for other in (core, 1 - core)
-    ] + [partner]
+    pair_grad = remote(sent_ref, pair_grad_ref, misc_send.at[3], misc_recv.at[3], partner)
+    side = chip - 1
+    chips_to = (CHIPS - 1 - mate_chip, CHIPS - 1 - chip, mate_chip)
 
     def grad_copy(n):
-        slot = me - CORES
         return remote(
-            sent_ref, held_ref.at[slot], grad_send.at[n], grad_recv.at[slot], places_to[n]
-        )
-
-    def grad_from(sender):
-        slot = sender - CORES
-        return remote(
-            sent_ref, held_ref.at[slot], grad_send.at[slot], grad_recv.at[slot], partner
-        )
+            both_ref, held_ref.at[side], grad_send.at[n], grad_recv.at[side],
+            chips_to[n] * CORES + core,
+        )
+
+    def grad_from(slot):
+        return remote(both_ref, held_ref.at[slot], grad_send.at[slot], grad_recv.at[slot], mate)
 
     @pl.when(outer)
     def _():
@@ -891,13 +886,17 @@
         mate_grad.wait_recv()
         pack_sent(jnp.concatenate(total, axis=1), mate_grad_ref[...].astype(F32))
         back_ref[...] = back
-        held_ref[me - CORES] = sent_ref[...]
 
     @pl.when(inner)
     def _():
-        for n in range(devices - 1):
+        pair_grad.start()
+        back_copy.start()
+        pair_grad.wait_recv()
+        both = (sent_ref[...].astype(F32) + pair_grad_ref[...].astype(F32)).astype(BF16)
+        both_ref[...] = both
+        held_ref[side] = both
+        for n in range(len(chips_to)):
             grad_copy(n).start()
-        back_copy.start()
 
     def put_terms(places):
         terms = exact(places, match_ref[...], (((1,), (1,)), ((), ())))
@@ -908,9 +907,9 @@
     def _():
         put_terms(places)
 
-    senders = range(CORES, devices - CORES)
+    senders = range(CHIPS - 2)
     for sender in senders:
-        @pl.when(me != sender)
+        @pl.when(side != sender)
         def _():
             grad_from(sender).wait_recv()
 
@@ -939,7 +938,8 @@
     @pl.when(inner)
     def _():
         back_copy.wait_send()
-        for n in range(devices - 1):
+        pair_grad.wait_send()
+        for n in range(len(chips_to)):
             grad_copy(n).wait_send()
 
 
@@ -999,7 +999,9 @@
         pltpu.VMEM((tilt_dev, 2 * node_count), F32),
         pltpu.VMEM((2 * node_count // pixels * tilt_dev, pixels), BF16),
         pltpu.VMEM((2 * node_count // pixels * tilt_dev, pixels), BF16),
-        pltpu.VMEM((devices - 2 * CORES, 2 * node_count // pixels * tilt_dev, pixels), BF16),
+        pltpu.VMEM((2 * node_count // pixels * tilt_dev, pixels), BF16),
+        pltpu.VMEM((2 * node_count // pixels * tilt_dev, pixels), BF16),
+        pltpu.VMEM((CHIPS - 2, 2 * node_count // pixels * tilt_dev, pixels), BF16),
         pltpu.VMEM((8, pixels), F32),
         pltpu.VMEM((8, pixels), F32),
         dma((chunks + 3,)),
@@ -1008,10 +1010,10 @@
         dma((8, chunks)),
         dma((guest_chunks,)),
         dma((guest_chunks,)),
+        dma((4,)),
+        dma((4,)),
         dma((3,)),
-        dma((3,)),
-        dma((devices - 1,)),
-        dma((devices - 2 * CORES,)),
+        dma((CHIPS - 2,)),
     ]
     terms, new_warp = pl.pallas_call(
         functools.partial(gather_kernel, cap, view_dev, bounds, guest_bounds),

time: 79.6 us -> 79.7 us (level)
  no operation moved by 1% of the time
where the time goes in v5:
time: 79.7 us; the launch traced here: 79.5 us
  Pallas kernels  77.7 us (97%)
  local copies, waits for them, and re-layouts  1.17 us (1%)
    pallas_call x1, Pallas kernels, on_device_gathered(): pl.pallas_call(functools.partial(gather_kernel, cap, view_dev, bounds, gu...  77.7 us

profile of v5, /device:TPU:0, one launch (start us, length us, event | category | flops | bytes accessed | tf_op | source)
XLA Modules:
  0.0 79.5 jit_solution(9991914047102605106)
XLA Ops:
  0.6 77.7 %gather_sums.1 = (f32[3,1,128]{2,1,0:T(1,128)S(1)}, f32[10,2,256]{2,1,0:T(2,128)S(1)}) custom-call(s32[1,128]{1,0:T(1,128)} %bitcast.6, s32[1,128]{1,0:T(1,128)} %tilt_ref.1, bf16[2,128]{1,0:T(2,128)(2,1)} %bitcast.7, bf16[1,128]{1,0:T(2,128)(2,1)} %focus_ref.1, f32[10,2,256]{2,1,0:T(2,128)} %warp_ref.1, bf16[128,128,128]{2,1,0:T(8,128)(2,1)} %bitcast.4, ...), custom_call_target="tpu_custom_call" | custom-call | tf_op jit(solution)/shard_map/gather_sums/pallas_call | solution.py:1018
  78.3 0.6 copy.19
  78.9 0.6 copy.20
